TPU v7x, 32 devices: a whole 2x2x4 slice. The times are simulated.
32 devices in a mesh: parts: 2 (over y), step: 4 (over z), frame: 2 (over x), head: 2 (over core).
Axes of the slice: x: 2, y: 2, z: 4, core: 2. Of those that a mesh axis runs over, the one named last changes fastest.
Arguments:
- start_noise: float32 [32, 256], P('parts', 'frame'), parts along dimension 0, may hold values from -6 to 6
- position: bfloat16 [256, 1152], P('frame'), may hold values from -6 to 6
- time_table: bfloat16 [128, 1152], replicated, may hold values from -6 to 6
- time_index: int32 [4], P('step'), may hold values from 0 to 127
- sched_index: int32 [4], P('step'), may hold values from 0 to 127
- coef_keep: float32 [128], replicated, may hold values from -0.06 to -0.01
- coef_noise: float32 [128], replicated, may hold values from 0.03 to 0.12
- w_in: bfloat16 [16, 1152], replicated, may hold values from -1.5 to 1.5
- norm_gain: float32 [1152], replicated, may hold values from 0.5 to 1.5
- w_qkv: bfloat16 [1152, 3, 1152], P('step', None, 'head'), may hold values from -4 to 4
- w_proj: bfloat16 [1152, 1152], P('step', 'head'), may hold values from -0.1875 to 0.1875
- w_final: bfloat16 [16, 1152], replicated, may hold values from -0.1875 to 0.1875
Outputs:
- trajectory: float32 [4, 32, 256], P('step', 'parts', 'frame'), parts along dimension 1
- residual_norms: float32 [8], P('parts'), parts along dimension 0
There are 2 independent parts, one for each index of `parts`. A program takes and returns all parts, laid end to end along the dimension named above; an argument that names none is the same for every part. Nothing has to cross between parts.
All inputs are finite; a program needn't handle non-finite values.
Results may differ from a plain program's by a relative error of at most 0.0044.
Values may be sent and summed in bfloat16 or wider, within the bound.
A program may use at most 64 MiB of HBM per device.

v0:
```python
import functools
import math

import jax
import jax.numpy as jnp
from jax import lax
from jax.experimental import pallas as pl
from jax.experimental.pallas import tpu as pltpu
from jax.sharding import PartitionSpec as P

HDIM = 72
ITERS = 4


def entering(value, axis, combine, identity):
    count, here = (lax.axis_size(axis), lax.axis_index(axis))
    everything = lax.all_gather(value, axis)
    start = jnp.broadcast_to(jnp.asarray(identity, value.dtype), value.shape)

    def hop(k, before):
        reached = k < here
        new = combine(before, everything[k])
        return jnp.where(reached, new, before)

    return lax.fori_loop(0, count, hop, start)


def add_terms(first, second):
    return first + second


def local_any(
    start_noise,
    position,
    time_table,
    time_index,
    sched_index,
    coef_keep,
    coef_noise,
    w_in,
    norm_gain,
    w_qkv,
    w_proj,
    w_final,
):
    w_qkv_all, w_proj_all = (
        lax.all_gather(w_qkv, "step", axis=0, tiled=True),
        lax.all_gather(w_proj, "step", axis=0, tiled=True),
    )
    batch_steps = time_index.shape[0]
    row_count = start_noise.shape[1]
    table_rows = time_table.shape[0]
    pick_time = (time_index[:, None] == jnp.arange(table_rows)[None, :]).astype(jnp.bfloat16)
    time_embed = jnp.dot(pick_time, time_table, preferred_element_type=jnp.float32)
    pick_sched = (sched_index[:, None] == jnp.arange(table_rows)[None, :]).astype(jnp.float32)
    keep_rate = jnp.sum(pick_sched * coef_keep[None, :], axis=1)
    noise_rate = jnp.sum(pick_sched * coef_noise[None, :], axis=1)
    heads_local = w_qkv_all.shape[2] // HDIM
    cell_count = (
        batch_steps
        * lax.axis_size("step")
        * start_noise.shape[0]
        * row_count
        * lax.axis_size("frame")
    )
    states = start_noise[None]
    drift_term = jnp.zeros_like(states)
    residual_list = []
    for iteration in range(ITERS):
        latent_bf = states.astype(jnp.bfloat16)
        hidden = (
            jnp.einsum("bcr,cd->brd", latent_bf, w_in, preferred_element_type=jnp.float32)
            + position
            + time_embed[:, None, :]
        )
        normed = (
            hidden * lax.rsqrt(jnp.mean(hidden * hidden, axis=2, keepdims=True) + 1e-06) * norm_gain
        ).astype(jnp.bfloat16)
        projected = jnp.einsum(
            "brd,dkq->brkq", normed, w_qkv_all, preferred_element_type=jnp.float32
        ).astype(jnp.bfloat16)
        queries = projected[:, :, 0].reshape(batch_steps, row_count, heads_local, HDIM)
        score_scale = 1.0 / math.sqrt(HDIM)
        keys_values = projected[:, :, 1:3]
        piece = lax.all_gather(keys_values, "frame", axis=1, tiled=True)
        top_old = jnp.full((batch_steps, heads_local, row_count), -1e30, jnp.float32)
        piece_rows = piece.shape[1]
        keys_blk = piece[:, :, 0].reshape(batch_steps, piece_rows, heads_local, HDIM)
        values_blk = piece[:, :, 1].reshape(batch_steps, piece_rows, heads_local, HDIM)
        scores = (
            jnp.einsum("bqhe,bkhe->bhqk", queries, keys_blk, preferred_element_type=jnp.float32)
            * score_scale
        )
        top_new = jnp.maximum(top_old, jnp.max(scores, axis=3))
        weights_exp = jnp.exp(scores - top_new[:, :, :, None])
        total_new = jnp.sum(weights_exp, axis=3)
        update = jnp.einsum(
            "bhqk,bkhe->bqhe",
            weights_exp.astype(jnp.bfloat16),
            values_blk,
            preferred_element_type=jnp.float32,
        )
        accum = update
        top_final, total_final, accum = (top_new, total_new, accum)
        attended = accum / jnp.transpose(total_final, (0, 2, 1))[:, :, :, None]
        attn_mixed = attended.reshape(batch_steps, row_count, heads_local * HDIM).astype(
            jnp.bfloat16
        )
        partial_value = jnp.einsum(
            "brq,dq->brd", attn_mixed, w_proj_all, preferred_element_type=jnp.float32
        )
        head_total = lax.psum(partial_value, "head")
        joined = (hidden + head_total).astype(jnp.bfloat16)
        predicted = jnp.einsum("cd,brd->bcr", w_final, joined, preferred_element_type=jnp.float32)
        drift_term = keep_rate[:, None, None] * states + noise_rate[:, None, None] * predicted
        local_incl = jnp.cumsum(drift_term, axis=0)
        local_total = local_incl[-1]
        earlier = entering(local_total, "step", add_terms, jnp.zeros_like(local_total))
        before = earlier[None] + (local_incl - drift_term)
        new_states = start_noise[None] + before
        change = new_states - states
        square_sum = jnp.sum(change * change)
        summed = lax.psum(square_sum, ("step", "frame"))
        residual_list.append(jnp.sqrt(summed / cell_count + 1e-06))
        states = new_states
    residual_norms = jnp.stack(residual_list)
    trajectory = states + drift_term
    return (trajectory, residual_norms)


MESH = pl.DeviceIdType.MESH
F32 = jnp.float32
BF16 = jnp.bfloat16


def dot(a, b, ca=1, cb=0):
    return lax.dot_general(a, b, (((ca,), (cb,)), ((), ())), preferred_element_type=F32)


def dot_exact(a, b):
    return lax.dot_general(
        a, b, (((1,), (0,)), ((), ())), precision=lax.Precision.HIGHEST, preferred_element_type=F32
    )


def two(a):
    high = a.astype(BF16)
    return high, (a - high.astype(F32)).astype(BF16)


def evals_of(steps):
    return [(i, j) for j in range(steps - 1) for i in range(min(j, ITERS - 1) + 1)] + [
        (min(ITERS, steps) - 1, steps - 1)
    ]


def kernel(
    S,
    F,
    H,
    noise_hbm,
    pos_hbm,
    table_hbm,
    tidx_ref,
    sidx_ref,
    keep_hbm,
    coef_hbm,
    win_hbm,
    gain_hbm,
    wqkv_hbm,
    wproj_hbm,
    wfin_hbm,
    traj_ref,
    res_ref,
    table_ref,
    keep_ref,
    coef_ref,
    win_ref,
    gain_ref,
    wqkv_ref,
    wproj_ref,
    wfin_ref,
    w_buf,
    m_buf,
    pos_buf,
    noise_buf,
    meta_buf,
    base_buf,
    plane_buf,
    line_buf,
    wsend_ref,
    msend_ref,
    ssem,
    rsem,
):
    s, f, h = (lax.axis_index(a) for a in ("step", "frame", "head"))
    loads = [
        pltpu.make_async_copy(src, dst, ssem.at[ssem.shape[0] - 1 - n])
        for n, (src, dst) in enumerate(
            (
                (pos_hbm, pos_buf.at[f]),
                (noise_hbm, noise_buf.at[f]),
                (keep_hbm, keep_ref),
                (coef_hbm, coef_ref),
                (wqkv_hbm, wqkv_ref),
                (wproj_hbm, wproj_ref),
                (wfin_hbm, wfin_ref),
                (table_hbm, table_ref),
                (win_hbm, win_ref),
                (gain_hbm, gain_ref),
            )
        )
    ]
    for copy in loads:
        copy.start()
    PL = F * H
    q_me = f * H + h
    C, rows = noise_buf.shape[1:]
    D = pos_buf.shape[2]
    N = rows * F
    pad = w_buf.shape[2]
    lanes = table_ref.shape[0]

    def step_peer(d):
        return {"step": lax.rem(s + d, S)}

    def plane_peer(d):
        t = lax.rem(q_me + d, PL)
        return {"frame": t // H, "head": lax.rem(t, H)}

    def frame_peer(d):
        return {"frame": lax.rem(f + d, F)}

    barrier = pltpu.get_barrier_semaphore()
    for d in range(1, S):
        pl.semaphore_signal(barrier, inc=1, device_id=step_peer(d), device_id_type=MESH)
    for d in range(1, PL):
        pl.semaphore_signal(barrier, inc=1, device_id=plane_peer(d), device_id_type=MESH)

    for copy in loads[:4]:
        copy.wait()
    row_id = lax.broadcasted_iota(jnp.int32, (8, lanes), 0)
    lane_id = lax.broadcasted_iota(jnp.int32, (1, lanes), 1)
    hot_t = jnp.where(lane_id == tidx_ref[0], 1.0, 0.0)
    hot_s = lane_id == sidx_ref[0]
    keep = jnp.sum(jnp.where(hot_s, keep_ref[...], 0.0), axis=1, keepdims=True)
    coef = jnp.sum(jnp.where(hot_s, coef_ref[...], 0.0), axis=1, keepdims=True)
    meta_buf[s] = jnp.where(row_id == 0, hot_t, jnp.where(row_id == 1, keep, coef))
    pl.semaphore_wait(barrier, S - 1 + PL - 1)

    count = [0]
    started = []

    def send(src, dst, peer):
        k = count[0]
        count[0] += 1
        copy = pltpu.make_async_remote_copy(
            src_ref=src,
            dst_ref=dst,
            send_sem=ssem.at[k],
            recv_sem=rsem.at[k],
            device_id=peer,
            device_id_type=MESH,
        )
        copy.start()
        started.append(copy)
        return copy

    order = sorted(range(1, S), key=lambda d: abs(d - S / 2))
    early = [send(meta_buf.at[s], meta_buf.at[s], step_peer(d)) for d in order]
    early += [send(noise_buf.at[f], noise_buf.at[f], frame_peer(d)) for d in range(1, F)]
    early += [send(pos_buf.at[f], pos_buf.at[f], frame_peer(d)) for d in range(1, F)]
    for copy in loads[4:7]:
        copy.wait()
    R = wqkv_ref.shape[1]
    for i in range(F):

        @pl.when(f == i)
        def _():
            for t in range(S):
                low = (t * F + i) * HDIM
                parts = [wqkv_ref[p, :, low : low + HDIM] for p in range(3)]
                parts.append(jnp.zeros((R, pad - 3 * HDIM), BF16))
                wsend_ref[t] = jnp.concatenate(parts, axis=1)

    late = [
        send(wsend_ref.at[lax.rem(s + d, S)], w_buf.at[s], step_peer(d)) for d in order
    ]
    rows_of = wfin_ref[:, 0:R].astype(F32)
    for j in range(1, S):
        rows_of = jnp.where(s == j, wfin_ref[:, j * R : (j + 1) * R].astype(F32), rows_of)
    folded = dot(rows_of.astype(BF16), wproj_ref[...])
    for t in range(S):
        picked = folded[:, t * F * HDIM : (t * F + 1) * HDIM]
        for i in range(1, F):
            low = (t * F + i) * HDIM
            picked = jnp.where(f == i, folded[:, low : low + HDIM], picked)
        msend_ref[t] = picked
    late += [
        send(msend_ref.at[lax.rem(s + d, S)], m_buf.at[s], step_peer(d)) for d in order
    ]
    w_buf[s] = wsend_ref[s]
    m_buf[s] = msend_ref[s]
    for copy in loads[7:]:
        copy.wait()
    for copy in early:
        copy.wait_recv()

    pos = pos_buf[...].reshape(N, D)
    start = jnp.concatenate([noise_buf[i] for i in range(F)], axis=1)
    metas = [meta_buf[j] for j in range(S)]
    hot = jnp.concatenate(
        [m[0:1] for m in metas] + [jnp.zeros((8 - S, lanes), F32)], axis=0
    ).astype(BF16)
    keeps = [jnp.concatenate([m[1:2, :rows]] * F, axis=1) for m in metas]
    coefs = [jnp.concatenate([m[2:3, :rows]] * F, axis=1) for m in metas]
    temb = dot(hot, table_ref[...])
    temb_b = temb.astype(BF16)
    gain = gain_ref[...]
    w_in = win_ref[...]
    posf = pos.astype(F32)
    p_hi, p_lo = two(posf * gain)
    side = jnp.concatenate(
        [w_in.astype(F32), temb, jnp.zeros((128 - C - 8, D), F32)], axis=0
    )
    q_hi, q_lo = two(side * gain)
    left = jnp.concatenate([p_hi, p_lo, q_hi, q_lo], axis=0)
    ends = jnp.concatenate([w_in, wfin_ref[...]], axis=0)
    ends_pos = dot(ends, pos, 1, 1)
    ends_t = dot(ends, temb_b, 1, 1)
    ends_in = dot(ends, w_in, 1, 1)
    sq_hi, sq_lo = two(posf * posf)
    ones = jnp.ones((8, D), BF16)
    norm_p = dot(ones, sq_hi, 1, 1) + dot(ones, sq_lo, 1, 1)
    cross = dot(temb_b, pos, 1, 1)
    norm_t = jnp.sum(temb * temb, axis=1, keepdims=True)
    norms = [norm_p[0:1] + 2.0 * cross[j : j + 1] + norm_t[j : j + 1] for j in range(S)]

    for copy in late:
        copy.wait_recv()

    wide = dot(left, w_buf[...].reshape(D, pad))
    by_pos = jnp.transpose(wide[0:N] + wide[N : 2 * N])
    by_side = jnp.transpose(wide[2 * N : 2 * N + 128] + wide[2 * N + 128 :])
    mix = m_buf[0]
    for j in range(1, S):
        mix = mix + m_buf[j]
    scale = 1.4426950408889634 / math.sqrt(HDIM)

    def table_of(t):
        return jnp.concatenate(
            [
                t[0:HDIM] * scale,
                t[HDIM : 2 * HDIM],
                dot_exact(mix, t[2 * HDIM : 3 * HDIM]),
            ],
            axis=0,
        )

    tab_pos, tab_side = table_of(by_pos), table_of(by_side)
    big_hi, big_lo = two(jnp.concatenate([tab_side[:, 0:C], ends_in], axis=0))
    for j in range(S):
        base_buf[j] = jnp.concatenate(
            [
                tab_pos + tab_side[:, C + j : C + j + 1],
                2.0 * (ends_pos[0:C] + ends_t[0:C, j : j + 1]),
                ends_pos[C : 2 * C] + ends_t[C : 2 * C, j : j + 1],
            ],
            axis=0,
        )
    QK = 2 * HDIM

    def partial(x, j):
        xb = x.astype(BF16)
        lin = dot(big_hi, xb) + dot(big_lo, xb) + base_buf[j]
        square = jnp.sum(xb.astype(F32) * lin[QK + C : QK + 2 * C], axis=0, keepdims=True)
        square = jnp.maximum(square + norms[j], 0.0)
        r = lax.rsqrt(square * (1.0 / D) + 1e-06)
        q = (lin[0:HDIM] * r).astype(BF16)
        k = (lin[HDIM:QK] * r).astype(BF16)
        v_hi, v_lo = two(lin[QK : QK + C] * r)
        scores = dot(k, q, 0, 0)
        e = jnp.exp2(scores - jnp.max(scores, axis=0, keepdims=True)).astype(BF16)
        o = dot(jnp.concatenate([v_hi, v_lo, jnp.ones((C, N), BF16)], axis=0), e)
        out = (o[0:C] + o[C : 2 * C]) / o[2 * C : 2 * C + 1]
        return out, lin[QK + 2 * C : QK + 3 * C]

    keys = evals_of(S)
    state, local_eps, drift, flying = {}, {}, {}, {}

    def launch(key):
        i, j = key
        n = keys.index(key)
        x = start
        for m in range(j if i else 0):
            x = x + drift[(min(i - 1, m), m)]
        state[key] = x
        part, local_eps[key] = partial(x, j)
        plane_buf[n, q_me] = part.astype(BF16)
        slot = plane_buf.at[n, q_me]
        flying[key] = [send(slot, slot, plane_peer(d)) for d in range(1, PL)]

    def relay(key):
        n = keys.index(key)
        for copy in flying[key]:
            copy.wait_recv()
        total = plane_buf[n, 0].astype(F32)
        for i in range(1, PL):
            total = total + plane_buf[n, i].astype(F32)
        line_buf[n, s] = total.astype(BF16)
        slot = line_buf.at[n, s]
        flying[key] = [send(slot, slot, step_peer(d)) for d in order]

    def land(key):
        n, j = keys.index(key), key[1]
        for copy in flying[key]:
            copy.wait_recv()
        total = local_eps[key]
        for i in range(S):
            total = total + line_buf[n, i].astype(F32)
        drift[key] = keeps[j] * state[key] + coefs[j] * total

    for act, key in PLAN:
        {"launch": launch, "relay": relay, "land": land}[act](key)

    old = [start] * S
    norms_out = []
    for it in range(ITERS):
        new, run = [], start
        for j in range(S):
            new.append(run)
            if j < S - 1:
                run = run + drift[(min(it, j), j)]
        square = jnp.zeros((1, 1), F32)
        for j in range(S):
            change = new[j] - old[j]
            square = square + jnp.sum(
                jnp.sum(change * change, axis=0, keepdims=True), axis=1, keepdims=True
            )
        norms_out.append(jnp.sqrt(square / (S * C * N) + 1e-06))
        old = new
    lane = lax.broadcasted_iota(jnp.int32, res_ref.shape, 1)
    res = jnp.zeros(res_ref.shape, F32)
    for it in range(ITERS):
        res = jnp.where(lane == it, norms_out[it], res)
    res_ref[...] = res
    mine = jnp.zeros((C, N), F32)
    for j in range(S):
        mine = jnp.where(s == j, old[j] + drift[(min(ITERS - 1, j), j)], mine)
    half = mine[:, 0:rows]
    for i in range(1, F):
        half = jnp.where(f == i, mine[:, i * rows : (i + 1) * rows], half)
    traj_ref[0] = half
    for copy in started:
        copy.wait_send()


PLAN = (
    ("launch", (0, 0)),
    ("launch", (0, 1)),
    ("relay", (0, 0)),
    ("launch", (0, 2)),
    ("relay", (0, 1)),
    ("land", (0, 0)),
    ("launch", (1, 1)),
    ("relay", (0, 2)),
    ("relay", (1, 1)),
    ("land", (0, 1)),
    ("launch", (1, 2)),
    ("land", (1, 1)),
    ("launch", (2, 2)),
    ("relay", (1, 2)),
    ("relay", (2, 2)),
    ("land", (0, 2)),
    ("land", (1, 2)),
    ("land", (2, 2)),
    ("launch", (3, 3)),
    ("relay", (3, 3)),
    ("land", (3, 3)),
)


def local_heads(
    start_noise,
    position,
    time_table,
    time_index,
    sched_index,
    coef_keep,
    coef_noise,
    w_in,
    norm_gain,
    w_qkv,
    w_proj,
    w_final,
):
    S, F, H = (lax.axis_size(a) for a in ("step", "frame", "head"))
    R = w_qkv.shape[0]
    C, rows = start_noise.shape
    D = position.shape[1]
    N = rows * F
    PL = F * H
    pad = -(-3 * HDIM // 128) * 128
    n_evals = len(evals_of(S))
    n_sems = 3 * (S - 1) + 2 * (F - 1) + n_evals * (PL - 1 + S - 1)
    vmem = pl.BlockSpec(memory_space=pltpu.VMEM)
    smem = pl.BlockSpec(memory_space=pltpu.SMEM)
    here = pl.BlockSpec(memory_space=pl.ANY)
    traj, res = pl.pallas_call(
        functools.partial(kernel, S, F, H),
        out_shape=(
            jax.ShapeDtypeStruct((1, C, rows), F32),
            jax.ShapeDtypeStruct((1, ITERS), F32),
        ),
        in_specs=[here, here, here, smem, smem] + [here] * 7,
        out_specs=(vmem, vmem),
        scratch_shapes=[
            pltpu.VMEM(time_table.shape, BF16),
            pltpu.VMEM((1, coef_keep.shape[0]), F32),
            pltpu.VMEM((1, coef_noise.shape[0]), F32),
            pltpu.VMEM(w_in.shape, BF16),
            pltpu.VMEM((1, D), F32),
            pltpu.VMEM((3, R, w_qkv.shape[2]), BF16),
            pltpu.VMEM(w_proj.shape, BF16),
            pltpu.VMEM(w_final.shape, BF16),
            pltpu.VMEM((S, R, pad), BF16),
            pltpu.VMEM((S, C, HDIM), F32),
            pltpu.VMEM((F, rows, D), BF16),
            pltpu.VMEM((F, C, rows), F32),
            pltpu.VMEM((S, 8, time_table.shape[0]), F32),
            pltpu.VMEM((S, 2 * HDIM + 3 * C, N), F32),
            pltpu.VMEM((n_evals, PL, C, N), BF16),
            pltpu.VMEM((n_evals, S, C, N), BF16),
            pltpu.VMEM((S, R, pad), BF16),
            pltpu.VMEM((S, C, HDIM), F32),
            pltpu.SemaphoreType.DMA((n_sems + 10,)),
            pltpu.SemaphoreType.DMA((n_sems,)),
        ],
        compiler_params=pltpu.CompilerParams(
            collective_id=0, has_side_effects=True, vmem_limit_bytes=60 * 1024 * 1024
        ),
    )(
        start_noise,
        position,
        time_table,
        time_index,
        sched_index,
        coef_keep[None],
        coef_noise[None],
        w_in,
        norm_gain[None],
        jnp.transpose(w_qkv, (1, 0, 2)),
        w_proj,
        w_final,
    )
    return traj, res.reshape(ITERS)


def one_head_each(mesh, start_noise, time_index, w_qkv, time_table):
    S, F, H = (mesh.shape[a] for a in ("step", "frame", "head"))
    return (
        S == ITERS
        and time_index.shape[0] == S
        and w_qkv.shape[2] == S * F * H * HDIM
        and w_qkv.shape[0] % (16 * S) == 0
        and start_noise.shape[1] % (128 * F) == 0
        and start_noise.shape[1] // F <= time_table.shape[0]
        and time_table.shape[0] % 128 == 0
    )


def solution(mesh):
    def call(*args):
        fits = one_head_each(mesh, args[0], args[3], args[9], args[2])
        return jax.shard_map(
            local_heads if fits else local_any,
            mesh=mesh,
            in_specs=(
                P("parts", "frame"),
                P("frame", None),
                P(),
                P("step"),
                P("step"),
                P(),
                P(),
                P(),
                P(),
                P("step", None, "head"),
                P("step", "head"),
                P(),
            ),
            out_specs=(P("step", "parts", "frame"), P("parts")),
            check_vma=False,
        )(*args)

    return call
```

profile of v0, /device:TPU:0, one launch (start us, length us, event | category | flops | bytes accessed | tf_op | source)
XLA Modules:
  0.0 57.6 jit_solution(1970917979121021677)
XLA Ops:
  1.9 1.3 %broadcast_in_dim.11.gain_hbm = f32[1,1152]{1,0:T(1,128)} reshape(f32[1152]{0:T(1024)} %param.20) | data formatting | bytes 9216 | tf_op jit(solution)/shard_map/broadcast_in_dim | solution.py:551
  3.2 51.9 %shard_map.131 = (f32[1,16,128]{2,1,0:T(8,128)}, f32[1,4]{1,0:T(1,128)}) custom-call(f32[16,128]{1,0:T(8,128)} %noise_hbm.1, bf16[128,1152]{1,0:T(8,128)(2,1)} %pos_hbm.1, bf16[128,1152]{1,0:T(8,128)(2,1)} %table_hbm.1, s32[1]{0:T(128)S(6)} %copy.16.tidx_ref, s32[1]{0:T(128)S(6)} %copy.17.sidx_ref, f32[1,128]{1,0:T(1,128)} %bitcast.5, f32[1,128]{1,0:T(1,128)} %bitcast.6, ...), custom_call_target="tpu_custom_call" | custom-call | tf_op jit(solution)/shard_map/pallas_call | solution.py:509
  55.1 1.3 %copy.18 = f32[1,16,128]{2,1,0:T(8,128)} copy(f32[1,16,128]{2,1,0:T(8,128)} %get-tuple-element.8) | data formatting | bytes 16384
  56.4 1.1 %copy.19 = f32[4]{0:T(128)} copy(f32[4]{0:T(128)} %bitcast.7) | data formatting | bytes 32
where the time goes:
time: 57.9 us; the launch traced here: 57.6 us
  Pallas kernels  51.9 us (90%)
  local copies, waits for them, and re-layouts  3.73 us (6%)
  between operations  1.93 us (3%)
    pallas_call x1, Pallas kernels, local_heads(): pl.pallas_call(functools.partial(kernel, S, F, H), out_shape=(jax.ShapeDt...  51.9 us
    unnamed x2, local copies, waits for them, and re-layouts  2.43 us
    broadcast_in_dim x1, local copies, waits for them, and re-layouts, local_heads(): norm_gain[None]  1.29 us

commit v1 on v0

--- a/solution.py
+++ b/solution.py
@@ -172,6 +172,7 @@
     wfin_hbm,
     traj_ref,
     res_ref,
+    pos_ref,
     table_ref,
     keep_ref,
     coef_ref,
@@ -180,16 +181,24 @@
     wqkv_ref,
     wproj_ref,
     wfin_ref,
-    w_buf,
-    m_buf,
-    pos_buf,
+    wt_ref,
+    at_ref,
+    at_peer,
+    side_ref,
+    pv_ref,
+    own_ref,
+    near_send,
+    near_recv,
+    far_send,
+    far_recv,
+    mix_send,
+    mix_buf,
     noise_buf,
     meta_buf,
+    ends_buf,
+    tab_buf,
     base_buf,
     plane_buf,
-    line_buf,
-    wsend_ref,
-    msend_ref,
     ssem,
     rsem,
 ):
@@ -198,16 +207,16 @@
         pltpu.make_async_copy(src, dst, ssem.at[ssem.shape[0] - 1 - n])
         for n, (src, dst) in enumerate(
             (
-                (pos_hbm, pos_buf.at[f]),
-                (noise_hbm, noise_buf.at[f]),
+                (gain_hbm, gain_ref),
+                (pos_hbm, pos_ref),
+                (wqkv_hbm, wqkv_ref),
+                (wfin_hbm, wfin_ref),
+                (wproj_hbm, wproj_ref),
                 (keep_hbm, keep_ref),
                 (coef_hbm, coef_ref),
-                (wqkv_hbm, wqkv_ref),
-                (wproj_hbm, wproj_ref),
-                (wfin_hbm, wfin_ref),
+                (noise_hbm, noise_buf.at[f]),
                 (table_hbm, table_ref),
                 (win_hbm, win_ref),
-                (gain_hbm, gain_ref),
             )
         )
     ]
@@ -216,37 +225,35 @@
     PL = F * H
     q_me = f * H + h
     C, rows = noise_buf.shape[1:]
-    D = pos_buf.shape[2]
+    D = pos_ref.shape[1]
     N = rows * F
-    pad = w_buf.shape[2]
+    R = wqkv_ref.shape[1]
     lanes = table_ref.shape[0]
+    e = lax.rem(s, 2)
+    e_near = 1 - e
+    s_near = s + 1 - 2 * e
+    s_far = lax.rem(s + 2, S)
+    HZ = wqkv_ref.shape[2] // (F * 2 * HDIM)
+    B = HZ * HDIM
+    QK = 2 * B
+    V = HZ * C
 
     def step_peer(d):
         return {"step": lax.rem(s + d, S)}
 
-    def plane_peer(d):
-        t = lax.rem(q_me + d, PL)
-        return {"frame": t // H, "head": lax.rem(t, H)}
-
-    def frame_peer(d):
-        return {"frame": lax.rem(f + d, F)}
+    def group_peer(d):
+        t = lax.rem(q_me + lax.rem(d, PL), PL)
+        z = s_near if d >= PL else s
+        return {"step": z, "frame": t // H, "head": lax.rem(t, H)}
+
+    frame_peer = {"frame": 1 - f}
 
     barrier = pltpu.get_barrier_semaphore()
     for d in range(1, S):
         pl.semaphore_signal(barrier, inc=1, device_id=step_peer(d), device_id_type=MESH)
-    for d in range(1, PL):
-        pl.semaphore_signal(barrier, inc=1, device_id=plane_peer(d), device_id_type=MESH)
-
-    for copy in loads[:4]:
-        copy.wait()
-    row_id = lax.broadcasted_iota(jnp.int32, (8, lanes), 0)
-    lane_id = lax.broadcasted_iota(jnp.int32, (1, lanes), 1)
-    hot_t = jnp.where(lane_id == tidx_ref[0], 1.0, 0.0)
-    hot_s = lane_id == sidx_ref[0]
-    keep = jnp.sum(jnp.where(hot_s, keep_ref[...], 0.0), axis=1, keepdims=True)
-    coef = jnp.sum(jnp.where(hot_s, coef_ref[...], 0.0), axis=1, keepdims=True)
-    meta_buf[s] = jnp.where(row_id == 0, hot_t, jnp.where(row_id == 1, keep, coef))
-    pl.semaphore_wait(barrier, S - 1 + PL - 1)
+    for d in range(1, 2 * PL):
+        if d != PL:
+            pl.semaphore_signal(barrier, inc=1, device_id=group_peer(d), device_id_type=MESH)
 
     count = [0]
     started = []
@@ -266,48 +273,88 @@
         started.append(copy)
         return copy
 
-    order = sorted(range(1, S), key=lambda d: abs(d - S / 2))
-    early = [send(meta_buf.at[s], meta_buf.at[s], step_peer(d)) for d in order]
-    early += [send(noise_buf.at[f], noise_buf.at[f], frame_peer(d)) for d in range(1, F)]
-    early += [send(pos_buf.at[f], pos_buf.at[f], frame_peer(d)) for d in range(1, F)]
-    for copy in loads[4:7]:
+    for copy in loads[:2]:
         copy.wait()
-    R = wqkv_ref.shape[1]
+    gain = gain_ref[...].reshape(1, D)
+    pos = pos_ref[...]
+    at_ref[...] = jnp.transpose(pos.astype(F32) * gain).astype(BF16)
+    loads[2].wait()
     for i in range(F):
 
         @pl.when(f == i)
         def _():
-            for t in range(S):
-                low = (t * F + i) * HDIM
-                parts = [wqkv_ref[p, :, low : low + HDIM] for p in range(3)]
-                parts.append(jnp.zeros((R, pad - 3 * HDIM), BF16))
-                wsend_ref[t] = jnp.concatenate(parts, axis=1)
-
-    late = [
-        send(wsend_ref.at[lax.rem(s + d, S)], w_buf.at[s], step_peer(d)) for d in order
-    ]
+            for p in range(3):
+                turned = jnp.transpose(wqkv_ref[p, :, i * 2 * B : (i + 1) * 2 * B])
+                for t in range(2):
+                    wt_ref[t, p * B : (p + 1) * B] = turned[t * B : (t + 1) * B]
+
+    mine = pl.ds(pl.multiple_of(s * R, R), R)
+    at_mine = at_ref[mine]
+    near_send[0] = dot(wt_ref[e_near, 0:QK], at_mine).astype(BF16)
+    loads[3].wait()
+    loads[4].wait()
     rows_of = wfin_ref[:, 0:R].astype(F32)
     for j in range(1, S):
         rows_of = jnp.where(s == j, wfin_ref[:, j * R : (j + 1) * R].astype(F32), rows_of)
     folded = dot(rows_of.astype(BF16), wproj_ref[...])
-    for t in range(S):
-        picked = folded[:, t * F * HDIM : (t * F + 1) * HDIM]
-        for i in range(1, F):
-            low = (t * F + i) * HDIM
-            picked = jnp.where(f == i, folded[:, low : low + HDIM], picked)
-        msend_ref[t] = picked
-    late += [
-        send(msend_ref.at[lax.rem(s + d, S)], m_buf.at[s], step_peer(d)) for d in order
-    ]
-    w_buf[s] = wsend_ref[s]
-    m_buf[s] = msend_ref[s]
-    for copy in loads[7:]:
+    picked = folded[:, 0 : 2 * B]
+    for i in range(1, F):
+        picked = jnp.where(f == i, folded[:, i * 2 * B : (i + 1) * 2 * B], picked)
+    mix_buf[s] = picked.astype(BF16)
+    for copy in loads[5:8]:
         copy.wait()
+    row_id = lax.broadcasted_iota(jnp.int32, (8, lanes), 0)
+    lane_id = lax.broadcasted_iota(jnp.int32, (1, lanes), 1)
+    hot_t = jnp.where(lane_id == tidx_ref[0], 1.0, 0.0)
+    hot_s = lane_id == sidx_ref[0]
+    keep = jnp.sum(jnp.where(hot_s, keep_ref[...], 0.0), axis=1, keepdims=True)
+    coef = jnp.sum(jnp.where(hot_s, coef_ref[...], 0.0), axis=1, keepdims=True)
+    meta_buf[s] = jnp.where(row_id == 0, hot_t, jnp.where(row_id == 1, keep, coef))
+
+    pl.semaphore_wait(barrier, S - 1 + 2 * PL - 2)
+    near = [send(near_send.at[0], near_recv.at[0], {"step": s_near})]
+    turn = send(at_ref.at[mine], at_peer, frame_peer)
+    order = sorted(range(1, S), key=lambda d: abs(d - S / 2))
+    early = [send(meta_buf.at[s], meta_buf.at[s], step_peer(d)) for d in order]
+    early += [send(mix_buf.at[s], mix_buf.at[s], step_peer(d)) for d in order]
+    sides = [send(noise_buf.at[f], noise_buf.at[f], frame_peer)]
+
+    own_ref[0] = dot(wt_ref[e, 0:QK], at_mine)
+    pv_ref[0, :, 0:rows] = dot(wt_ref[e, QK : QK + B], at_mine).astype(BF16)
+    pv_ref[1, :, 0:rows] = dot(wt_ref[e_near, QK : QK + B], at_mine).astype(BF16)
+    for copy in loads[8:]:
+        copy.wait()
+    w_in = win_ref[...]
+    ends = jnp.concatenate([w_in, wfin_ref[...]], axis=0)
+    ends_in = dot(ends, w_in, 1, 1)
+    posf = pos.astype(F32)
+    sq_hi, sq_lo = two(posf * posf)
+    ones = jnp.ones((8, D), BF16)
+    ends_buf[f, 0 : 2 * C] = dot(ends, pos, 1, 1)
+    ends_buf[f, 2 * C : 2 * C + 8] = dot(ones, sq_hi, 1, 1) + dot(ones, sq_lo, 1, 1)
+
+    far = []
+
+    def pass_on(i, low, high):
+        near[i].wait_recv()
+        total = own_ref[i, low:high] + near_recv[i, low:high].astype(F32)
+        far_send[i, low:high] = total.astype(BF16)
+        window = pl.ds(low, high - low)
+        far.append(
+            send(far_send.at[i, window], far_recv.at[i, window], {"step": s_far})
+        )
+
+    pass_on(0, 0, QK)
+    turn.wait_recv()
+    at_other = at_peer[...]
+    near_send[1] = dot(wt_ref[e_near, 0:QK], at_other).astype(BF16)
+    near.append(send(near_send.at[1], near_recv.at[1], {"step": s_near}))
+    own_ref[1] = dot(wt_ref[e, 0:QK], at_other)
+    pv_ref[0, :, rows : 2 * rows] = dot(wt_ref[e, QK : QK + B], at_other).astype(BF16)
+    pv_ref[1, :, rows : 2 * rows] = dot(wt_ref[e_near, QK : QK + B], at_other).astype(BF16)
+
     for copy in early:
         copy.wait_recv()
-
-    pos = pos_buf[...].reshape(N, D)
-    start = jnp.concatenate([noise_buf[i] for i in range(F)], axis=1)
     metas = [meta_buf[j] for j in range(S)]
     hot = jnp.concatenate(
         [m[0:1] for m in metas] + [jnp.zeros((8 - S, lanes), F32)], axis=0
@@ -316,74 +363,119 @@
     coefs = [jnp.concatenate([m[2:3, :rows]] * F, axis=1) for m in metas]
     temb = dot(hot, table_ref[...])
     temb_b = temb.astype(BF16)
-    gain = gain_ref[...]
-    w_in = win_ref[...]
-    posf = pos.astype(F32)
-    p_hi, p_lo = two(posf * gain)
+    ends_buf[f, 2 * C + 8 : 2 * C + 16] = dot(temb_b, pos, 1, 1)
+    sides.append(send(ends_buf.at[f], ends_buf.at[f], frame_peer))
+    ends_t = dot(ends, temb_b, 1, 1)
+    norm_t = jnp.sum(temb * temb, axis=1, keepdims=True)
     side = jnp.concatenate(
         [w_in.astype(F32), temb, jnp.zeros((128 - C - 8, D), F32)], axis=0
     )
-    q_hi, q_lo = two(side * gain)
-    left = jnp.concatenate([p_hi, p_lo, q_hi, q_lo], axis=0)
-    ends = jnp.concatenate([w_in, wfin_ref[...]], axis=0)
-    ends_pos = dot(ends, pos, 1, 1)
-    ends_t = dot(ends, temb_b, 1, 1)
-    ends_in = dot(ends, w_in, 1, 1)
-    sq_hi, sq_lo = two(posf * posf)
-    ones = jnp.ones((8, D), BF16)
-    norm_p = dot(ones, sq_hi, 1, 1) + dot(ones, sq_lo, 1, 1)
-    cross = dot(temb_b, pos, 1, 1)
-    norm_t = jnp.sum(temb * temb, axis=1, keepdims=True)
-    norms = [norm_p[0:1] + 2.0 * cross[j : j + 1] + norm_t[j : j + 1] for j in range(S)]
-
-    for copy in late:
+    side_ref[...] = jnp.transpose(side * gain).astype(BF16)
+    side_mine = side_ref[mine]
+    mix = mix_buf[0].astype(F32)
+    for j in range(1, S):
+        mix = mix + mix_buf[j].astype(F32)
+    mix_lane = lax.broadcasted_iota(jnp.int32, (V, B), 1) // HDIM
+    mix_row = lax.broadcasted_iota(jnp.int32, (V, B), 0) // C
+
+    def late_rows(role, member):
+        pv_ref[role, :, 2 * rows : 2 * rows + 128] = dot(
+            wt_ref[member, QK : QK + B], side_mine
+        ).astype(BF16)
+        part = jnp.where(member == 0, mix[:, 0:B], mix[:, B : 2 * B])
+        block = jnp.where(
+            mix_lane == mix_row, jnp.concatenate([part] * HZ, axis=0), 0.0
+        )
+        block_hi, block_lo = two(block)
+        values = dot(jnp.concatenate([block_hi, block_lo], axis=0), pv_ref[role])
+        values = values[0:V] + values[V : 2 * V]
+        turned = dot(wt_ref[member, 0:QK], side_mine)
+        packs = []
+        for arr in (turned, values[:, 2 * rows : 2 * rows + 128]):
+            size = arr.shape[0] // 4
+            packed = arr[0:size]
+            for g in range(1, 4):
+                packed = packed + pltpu.roll(arr[g * size : (g + 1) * size], 32 * g, 1)
+            packs.append(packed)
+        return jnp.concatenate(
+            [values[:, 0:rows], values[:, rows : 2 * rows]] + packs, axis=0
+        )
+
+    LATE = 2 * V + (QK + V) // 4
+    near_send[2, 0:LATE] = late_rows(1, e_near).astype(BF16)
+    tail_rows = pl.ds(0, LATE)
+    near.append(
+        send(near_send.at[2, tail_rows], near_recv.at[2, tail_rows], {"step": s_near})
+    )
+    own_ref[2, 0:LATE] = late_rows(0, e)
+    pass_on(1, 0, QK)
+    pass_on(2, 0, LATE)
+
+    scale = 1.4426950408889634 / math.sqrt(HDIM)
+    qk_row = lax.broadcasted_iota(jnp.int32, (QK, 1), 0)
+    row_scale = jnp.where(qk_row < B, scale, 1.0)
+
+    def whole(i, low, high):
+        return far_send[i, low:high].astype(F32) + far_recv[i, low:high].astype(F32)
+
+    far[0].wait_recv()
+    tab_buf[f, 0:QK] = whole(0, 0, QK) * row_scale
+    for copy in sides:
         copy.wait_recv()
-
-    wide = dot(left, w_buf[...].reshape(D, pad))
-    by_pos = jnp.transpose(wide[0:N] + wide[N : 2 * N])
-    by_side = jnp.transpose(wide[2 * N : 2 * N + 128] + wide[2 * N + 128 :])
-    mix = m_buf[0]
-    for j in range(1, S):
-        mix = mix + m_buf[j]
-    scale = 1.4426950408889634 / math.sqrt(HDIM)
-
-    def table_of(t):
-        return jnp.concatenate(
-            [
-                t[0:HDIM] * scale,
-                t[HDIM : 2 * HDIM],
-                dot_exact(mix, t[2 * HDIM : 3 * HDIM]),
-            ],
-            axis=0,
-        )
-
-    tab_pos, tab_side = table_of(by_pos), table_of(by_side)
-    big_hi, big_lo = two(jnp.concatenate([tab_side[:, 0:C], ends_in], axis=0))
+    start = jnp.concatenate([noise_buf[i] for i in range(F)], axis=1)
+    ends_all = jnp.concatenate([ends_buf[i] for i in range(F)], axis=1)
+    ends_pos = ends_all[0 : 2 * C]
+    norm_p = ends_all[2 * C : 2 * C + 1]
+    cross = ends_all[2 * C + 8 : 2 * C + 16]
+    norms = [norm_p + 2.0 * cross[j : j + 1] + norm_t[j : j + 1] for j in range(S)]
     for j in range(S):
         base_buf[j] = jnp.concatenate(
             [
-                tab_pos + tab_side[:, C + j : C + j + 1],
                 2.0 * (ends_pos[0:C] + ends_t[0:C, j : j + 1]),
                 ends_pos[C : 2 * C] + ends_t[C : 2 * C, j : j + 1],
             ],
             axis=0,
         )
-    QK = 2 * HDIM
+    far[1].wait_recv()
+    tab_buf[1 - f, 0:QK] = whole(1, 0, QK) * row_scale
+    far[2].wait_recv()
+    last = whole(2, 0, LATE)
+    tab_buf[f, QK : QK + V] = last[0:V]
+    tab_buf[1 - f, QK : QK + V] = last[V : 2 * V]
+    packed = last[2 * V : LATE]
+    size = QK // 4
+    big_qk = jnp.concatenate([packed[0:size, 32 * g : 32 * g + 32] for g in range(4)], axis=0)
+    big_v = jnp.concatenate([packed[size:, 32 * g : 32 * g + 32] for g in range(4)], axis=0)
+    ends_hi, ends_lo = two(
+        jnp.concatenate([ends_in, jnp.zeros((2 * C, 32 - C), F32)], axis=1)
+    )
+    big = jnp.concatenate(
+        [(big_qk * row_scale).astype(BF16), big_v.astype(BF16), ends_hi, ends_lo], axis=0
+    )
+    tab = jnp.concatenate([tab_buf[i] for i in range(F)], axis=1)
+    T = QK + V
+    hot_row = lax.broadcasted_iota(jnp.int32, (32 - C, N), 0)
 
     def partial(x, j):
         xb = x.astype(BF16)
-        lin = dot(big_hi, xb) + dot(big_lo, xb) + base_buf[j]
-        square = jnp.sum(xb.astype(F32) * lin[QK + C : QK + 2 * C], axis=0, keepdims=True)
+        pick = jnp.where(hot_row == j, 1.0, 0.0).astype(BF16)
+        lin = dot(big, jnp.concatenate([xb, pick], axis=0))
+        tail = lin[T : T + 2 * C] + lin[T + 2 * C : T + 4 * C]
+        base = base_buf[j]
+        square = jnp.sum(xb.astype(F32) * (tail[0:C] + base[0:C]), axis=0, keepdims=True)
         square = jnp.maximum(square + norms[j], 0.0)
         r = lax.rsqrt(square * (1.0 / D) + 1e-06)
-        q = (lin[0:HDIM] * r).astype(BF16)
-        k = (lin[HDIM:QK] * r).astype(BF16)
-        v_hi, v_lo = two(lin[QK : QK + C] * r)
-        scores = dot(k, q, 0, 0)
-        e = jnp.exp2(scores - jnp.max(scores, axis=0, keepdims=True)).astype(BF16)
-        o = dot(jnp.concatenate([v_hi, v_lo, jnp.ones((C, N), BF16)], axis=0), e)
-        out = (o[0:C] + o[C : 2 * C]) / o[2 * C : 2 * C + 1]
-        return out, lin[QK + 2 * C : QK + 3 * C]
+        lin = (lin[0:T] + tab) * r
+        out = jnp.zeros((C, N), F32)
+        for n in range(HZ):
+            q = lin[n * HDIM : (n + 1) * HDIM].astype(BF16)
+            k = lin[B + n * HDIM : B + (n + 1) * HDIM].astype(BF16)
+            v_hi, v_lo = two(lin[QK + n * C : QK + (n + 1) * C])
+            scores = dot(k, q, 0, 0)
+            p = jnp.exp2(scores - jnp.max(scores, axis=0, keepdims=True)).astype(BF16)
+            o = dot(jnp.concatenate([v_hi, v_lo, jnp.ones((C, N), BF16)], axis=0), p)
+            out = out + (o[0:C] + o[C : 2 * C]) / o[2 * C : 2 * C + 1]
+        return out, tail[C : 2 * C] + base[C : 2 * C]
 
     keys = evals_of(S)
     state, local_eps, drift, flying = {}, {}, {}, {}
@@ -396,32 +488,22 @@
             x = x + drift[(min(i - 1, m), m)]
         state[key] = x
         part, local_eps[key] = partial(x, j)
-        plane_buf[n, q_me] = part.astype(BF16)
-        slot = plane_buf.at[n, q_me]
-        flying[key] = [send(slot, slot, plane_peer(d)) for d in range(1, PL)]
-
-    def relay(key):
-        n = keys.index(key)
-        for copy in flying[key]:
-            copy.wait_recv()
-        total = plane_buf[n, 0].astype(F32)
-        for i in range(1, PL):
-            total = total + plane_buf[n, i].astype(F32)
-        line_buf[n, s] = total.astype(BF16)
-        slot = line_buf.at[n, s]
-        flying[key] = [send(slot, slot, step_peer(d)) for d in order]
+        own = e * PL + q_me
+        plane_buf[n, own] = part.astype(BF16)
+        slot = plane_buf.at[n, own]
+        flying[key] = [send(slot, slot, group_peer(d)) for d in range(1, 2 * PL)]
 
     def land(key):
         n, j = keys.index(key), key[1]
         for copy in flying[key]:
             copy.wait_recv()
         total = local_eps[key]
-        for i in range(S):
-            total = total + line_buf[n, i].astype(F32)
+        for i in range(2 * PL):
+            total = total + plane_buf[n, i].astype(F32)
         drift[key] = keeps[j] * state[key] + coefs[j] * total
 
     for act, key in PLAN:
-        {"launch": launch, "relay": relay, "land": land}[act](key)
+        {"launch": launch, "land": land}[act](key)
 
     old = [start] * S
     norms_out = []
@@ -444,12 +526,12 @@
     for it in range(ITERS):
         res = jnp.where(lane == it, norms_out[it], res)
     res_ref[...] = res
-    mine = jnp.zeros((C, N), F32)
+    final = jnp.zeros((C, N), F32)
     for j in range(S):
-        mine = jnp.where(s == j, old[j] + drift[(min(ITERS - 1, j), j)], mine)
-    half = mine[:, 0:rows]
+        final = jnp.where(s == j, old[j] + drift[(min(ITERS - 1, j), j)], final)
+    half = final[:, 0:rows]
     for i in range(1, F):
-        half = jnp.where(f == i, mine[:, i * rows : (i + 1) * rows], half)
+        half = jnp.where(f == i, final[:, i * rows : (i + 1) * rows], half)
     traj_ref[0] = half
     for copy in started:
         copy.wait_send()
@@ -458,24 +540,17 @@
 PLAN = (
     ("launch", (0, 0)),
     ("launch", (0, 1)),
-    ("relay", (0, 0)),
     ("launch", (0, 2)),
-    ("relay", (0, 1)),
     ("land", (0, 0)),
     ("launch", (1, 1)),
-    ("relay", (0, 2)),
-    ("relay", (1, 1)),
     ("land", (0, 1)),
     ("launch", (1, 2)),
     ("land", (1, 1)),
     ("launch", (2, 2)),
-    ("relay", (1, 2)),
-    ("relay", (2, 2)),
     ("land", (0, 2)),
     ("land", (1, 2)),
     ("land", (2, 2)),
     ("launch", (3, 3)),
-    ("relay", (3, 3)),
     ("land", (3, 3)),
 )
 
@@ -500,39 +575,48 @@
     D = position.shape[1]
     N = rows * F
     PL = F * H
-    pad = -(-3 * HDIM // 128) * 128
+    HZ = w_qkv.shape[2] // (F * 2 * HDIM)
+    B = HZ * HDIM
+    QK = 2 * B
+    V = HZ * C
     n_evals = len(evals_of(S))
-    n_sems = 3 * (S - 1) + 2 * (F - 1) + n_evals * (PL - 1 + S - 1)
+    n_sems = 2 * (S - 1) + 3 + 6 + n_evals * (2 * PL - 1)
     vmem = pl.BlockSpec(memory_space=pltpu.VMEM)
     smem = pl.BlockSpec(memory_space=pltpu.SMEM)
     here = pl.BlockSpec(memory_space=pl.ANY)
     traj, res = pl.pallas_call(
         functools.partial(kernel, S, F, H),
-        out_shape=(
-            jax.ShapeDtypeStruct((1, C, rows), F32),
-            jax.ShapeDtypeStruct((1, ITERS), F32),
-        ),
+        out_shape=(pltpu.VMEM((1, C, rows), F32), pltpu.VMEM((1, ITERS), F32)),
         in_specs=[here, here, here, smem, smem] + [here] * 7,
         out_specs=(vmem, vmem),
         scratch_shapes=[
+            pltpu.VMEM((rows, D), BF16),
             pltpu.VMEM(time_table.shape, BF16),
             pltpu.VMEM((1, coef_keep.shape[0]), F32),
             pltpu.VMEM((1, coef_noise.shape[0]), F32),
             pltpu.VMEM(w_in.shape, BF16),
-            pltpu.VMEM((1, D), F32),
+            pltpu.VMEM((D,), F32),
             pltpu.VMEM((3, R, w_qkv.shape[2]), BF16),
             pltpu.VMEM(w_proj.shape, BF16),
             pltpu.VMEM(w_final.shape, BF16),
-            pltpu.VMEM((S, R, pad), BF16),
-            pltpu.VMEM((S, C, HDIM), F32),
-            pltpu.VMEM((F, rows, D), BF16),
+            pltpu.VMEM((2, QK + B, R), BF16),
+            pltpu.VMEM((D, rows), BF16),
+            pltpu.VMEM((R, rows), BF16),
+            pltpu.VMEM((D, 128), BF16),
+            pltpu.VMEM((2, B, N + 128), BF16),
+            pltpu.VMEM((3, QK, rows), F32),
+            pltpu.VMEM((3, QK, rows), BF16),
+            pltpu.VMEM((3, QK, rows), BF16),
+            pltpu.VMEM((3, QK, rows), BF16),
+            pltpu.VMEM((3, QK, rows), BF16),
+            pltpu.VMEM((C, 2 * B), BF16),
+            pltpu.VMEM((S, C, 2 * B), BF16),
             pltpu.VMEM((F, C, rows), F32),
             pltpu.VMEM((S, 8, time_table.shape[0]), F32),
-            pltpu.VMEM((S, 2 * HDIM + 3 * C, N), F32),
-            pltpu.VMEM((n_evals, PL, C, N), BF16),
-            pltpu.VMEM((n_evals, S, C, N), BF16),
-            pltpu.VMEM((S, R, pad), BF16),
-            pltpu.VMEM((S, C, HDIM), F32),
+            pltpu.VMEM((F, 2 * C + 16, rows), F32),
+            pltpu.VMEM((F, QK + V, rows), F32),
+            pltpu.VMEM((S, 2 * C, N), F32),
+            pltpu.VMEM((n_evals, 2 * PL, C, N), BF16),
             pltpu.SemaphoreType.DMA((n_sems + 10,)),
             pltpu.SemaphoreType.DMA((n_sems,)),
         ],
@@ -548,7 +632,7 @@
         coef_keep[None],
         coef_noise[None],
         w_in,
-        norm_gain[None],
+        norm_gain,
         jnp.transpose(w_qkv, (1, 0, 2)),
         w_proj,
         w_final,

time: 57.9 us -> 41.1 us (0.71)
  Pallas kernels: 51.9 us -> 37.8 us
  local copies, waits for them, and re-layouts: 3.73 us -> 1.11 us
    pallas_call x1, Pallas kernels: 51.9 us -> 37.8 us  [local_heads(): pl.pallas_call(functools.partial(kernel, S, F, H), out_shape=(pltpu.VMEM(...]
    unnamed x2, local copies, waits for them, and re-layouts: 2.43 us -> 1.11 us
    broadcast_in_dim x1 -> x0, local copies, waits for them, and re-layouts: 1.29 us -> none  [local_heads(): norm_gain[None]]
where the time goes in v1:
time: 41.1 us; the launch traced here: 40.9 us
  Pallas kernels  37.8 us (92%)
  between operations  1.93 us (5%)
  local copies, waits for them, and re-layouts  1.11 us (3%)
    pallas_call x1, Pallas kernels, local_heads(): pl.pallas_call(functools.partial(kernel, S, F, H), out_shape=(pltpu.VMEM(...  37.8 us
    unnamed x2, local copies, waits for them, and re-layouts  1.11 us

profile of v1, /device:TPU:0, one launch (start us, length us, event | category | flops | bytes accessed | tf_op | source)
XLA Modules:
  0.0 40.9 jit_solution(10992528320233257622)
XLA Ops:
  1.9 37.8 %shard_map.131 = (f32[1,16,128]{2,1,0:T(8,128)S(1)}, f32[1,4]{1,0:T(1,128)S(1)}) custom-call(f32[16,128]{1,0:T(8,128)} %noise_hbm.1, bf16[128,1152]{1,0:T(8,128)(2,1)} %pos_hbm.1, bf16[128,1152]{1,0:T(8,128)(2,1)} %table_hbm.1, s32[1]{0:T(128)S(6)} %copy.18.tidx_ref, s32[1]{0:T(128)S(6)} %copy.19.sidx_ref, f32[1,128]{1,0:T(1,128)} %bitcast.6, ...), custom_call_target="tpu_custom_call" | custom-call | tf_op jit(solution)/shard_map/pallas_call | solution.py:587
  39.8 0.6 %copy.16 = f32[1,16,128]{2,1,0:T(8,128)} copy(f32[1,16,128]{2,1,0:T(8,128)S(1)} %get-tuple-element.6) | data formatting | bytes 16384
  40.4 0.5 %copy.17 = f32[4]{0:T(128)} copy(f32[4]{0:T(128)S(1)} %bitcast.4) | data formatting | bytes 32

commit v2 on v1

--- a/solution.py
+++ b/solution.py
@@ -185,13 +185,13 @@
     at_ref,
     at_peer,
     side_ref,
+    side_cut,
     pv_ref,
     own_ref,
     near_send,
     near_recv,
     far_send,
     far_recv,
-    mix_send,
     mix_buf,
     noise_buf,
     meta_buf,
@@ -207,13 +207,13 @@
         pltpu.make_async_copy(src, dst, ssem.at[ssem.shape[0] - 1 - n])
         for n, (src, dst) in enumerate(
             (
+                (keep_hbm, keep_ref),
+                (coef_hbm, coef_ref),
                 (gain_hbm, gain_ref),
                 (pos_hbm, pos_ref),
                 (wqkv_hbm, wqkv_ref),
                 (wfin_hbm, wfin_ref),
                 (wproj_hbm, wproj_ref),
-                (keep_hbm, keep_ref),
-                (coef_hbm, coef_ref),
                 (noise_hbm, noise_buf.at[f]),
                 (table_hbm, table_ref),
                 (win_hbm, win_ref),
@@ -249,11 +249,10 @@
     frame_peer = {"frame": 1 - f}
 
     barrier = pltpu.get_barrier_semaphore()
+    for d in range(1, PL):
+        pl.semaphore_signal(barrier, inc=1, device_id=group_peer(d), device_id_type=MESH)
     for d in range(1, S):
         pl.semaphore_signal(barrier, inc=1, device_id=step_peer(d), device_id_type=MESH)
-    for d in range(1, 2 * PL):
-        if d != PL:
-            pl.semaphore_signal(barrier, inc=1, device_id=group_peer(d), device_id_type=MESH)
 
     count = [0]
     started = []
@@ -273,12 +272,20 @@
         started.append(copy)
         return copy
 
-    for copy in loads[:2]:
+    for copy in loads[:3]:
+        copy.wait()
+    row_id = lax.broadcasted_iota(jnp.int32, (8, lanes), 0)
+    lane_id = lax.broadcasted_iota(jnp.int32, (1, lanes), 1)
+    hot_t = jnp.where(lane_id == tidx_ref[0], 1.0, 0.0)
+    hot_s = lane_id == sidx_ref[0]
+    keep = jnp.sum(jnp.where(hot_s, keep_ref[...], 0.0), axis=1, keepdims=True)
+    coef = jnp.sum(jnp.where(hot_s, coef_ref[...], 0.0), axis=1, keepdims=True)
+    meta_buf[s] = jnp.where(row_id == 0, hot_t, jnp.where(row_id == 1, keep, coef))
+    for copy in loads[3:5]:
         copy.wait()
     gain = gain_ref[...].reshape(1, D)
     pos = pos_ref[...]
     at_ref[...] = jnp.transpose(pos.astype(F32) * gain).astype(BF16)
-    loads[2].wait()
     for i in range(F):
 
         @pl.when(f == i)
@@ -291,8 +298,23 @@
     mine = pl.ds(pl.multiple_of(s * R, R), R)
     at_mine = at_ref[mine]
     near_send[0] = dot(wt_ref[e_near, 0:QK], at_mine).astype(BF16)
-    loads[3].wait()
-    loads[4].wait()
+    pl.semaphore_wait(barrier, S - 1 + PL - 1)
+    to_near, to_far = {"step": s_near}, {"step": s_far}
+    near, far = {}, {}
+
+    def send_near(i, low, high):
+        window = pl.ds(low, high - low)
+        near[i, low] = send(near_send.at[i, window], near_recv.at[i, window], to_near)
+
+    pieces = [(low, low + QK // 3) for low in range(0, QK, QK // 3)]
+    order = sorted(range(1, S), key=lambda d: abs(d - S / 2))
+    early = [send(meta_buf.at[s], meta_buf.at[s], step_peer(d)) for d in order]
+    send_near(0, *pieces[0])
+    turn = send(at_ref.at[mine], at_peer, frame_peer)
+    for piece in pieces[1:]:
+        send_near(0, *piece)
+    for copy in loads[5:7]:
+        copy.wait()
     rows_of = wfin_ref[:, 0:R].astype(F32)
     for j in range(1, S):
         rows_of = jnp.where(s == j, wfin_ref[:, j * R : (j + 1) * R].astype(F32), rows_of)
@@ -301,25 +323,20 @@
     for i in range(1, F):
         picked = jnp.where(f == i, folded[:, i * 2 * B : (i + 1) * 2 * B], picked)
     mix_buf[s] = picked.astype(BF16)
-    for copy in loads[5:8]:
-        copy.wait()
-    row_id = lax.broadcasted_iota(jnp.int32, (8, lanes), 0)
-    lane_id = lax.broadcasted_iota(jnp.int32, (1, lanes), 1)
-    hot_t = jnp.where(lane_id == tidx_ref[0], 1.0, 0.0)
-    hot_s = lane_id == sidx_ref[0]
-    keep = jnp.sum(jnp.where(hot_s, keep_ref[...], 0.0), axis=1, keepdims=True)
-    coef = jnp.sum(jnp.where(hot_s, coef_ref[...], 0.0), axis=1, keepdims=True)
-    meta_buf[s] = jnp.where(row_id == 0, hot_t, jnp.where(row_id == 1, keep, coef))
-
-    pl.semaphore_wait(barrier, S - 1 + 2 * PL - 2)
-    near = [send(near_send.at[0], near_recv.at[0], {"step": s_near})]
-    turn = send(at_ref.at[mine], at_peer, frame_peer)
-    order = sorted(range(1, S), key=lambda d: abs(d - S / 2))
-    early = [send(meta_buf.at[s], meta_buf.at[s], step_peer(d)) for d in order]
     early += [send(mix_buf.at[s], mix_buf.at[s], step_peer(d)) for d in order]
+    loads[7].wait()
     sides = [send(noise_buf.at[f], noise_buf.at[f], frame_peer)]
-
     own_ref[0] = dot(wt_ref[e, 0:QK], at_mine)
+
+    def pass_on(i, low, high):
+        near[i, low].wait_recv()
+        total = own_ref[i, low:high] + near_recv[i, low:high].astype(F32)
+        far_send[i, low:high] = total.astype(BF16)
+        window = pl.ds(low, high - low)
+        far[i, low] = send(far_send.at[i, window], far_recv.at[i, window], to_far)
+
+    for piece in pieces:
+        pass_on(0, *piece)
     pv_ref[0, :, 0:rows] = dot(wt_ref[e, QK : QK + B], at_mine).astype(BF16)
     pv_ref[1, :, 0:rows] = dot(wt_ref[e_near, QK : QK + B], at_mine).astype(BF16)
     for copy in loads[8:]:
@@ -333,26 +350,16 @@
     ends_buf[f, 0 : 2 * C] = dot(ends, pos, 1, 1)
     ends_buf[f, 2 * C : 2 * C + 8] = dot(ones, sq_hi, 1, 1) + dot(ones, sq_lo, 1, 1)
 
-    far = []
-
-    def pass_on(i, low, high):
-        near[i].wait_recv()
-        total = own_ref[i, low:high] + near_recv[i, low:high].astype(F32)
-        far_send[i, low:high] = total.astype(BF16)
-        window = pl.ds(low, high - low)
-        far.append(
-            send(far_send.at[i, window], far_recv.at[i, window], {"step": s_far})
-        )
-
-    pass_on(0, 0, QK)
     turn.wait_recv()
     at_other = at_peer[...]
     near_send[1] = dot(wt_ref[e_near, 0:QK], at_other).astype(BF16)
-    near.append(send(near_send.at[1], near_recv.at[1], {"step": s_near}))
+    for piece in pieces:
+        send_near(1, *piece)
     own_ref[1] = dot(wt_ref[e, 0:QK], at_other)
     pv_ref[0, :, rows : 2 * rows] = dot(wt_ref[e, QK : QK + B], at_other).astype(BF16)
     pv_ref[1, :, rows : 2 * rows] = dot(wt_ref[e_near, QK : QK + B], at_other).astype(BF16)
 
+    side_ref[0:C] = w_in.astype(F32)
     for copy in early:
         copy.wait_recv()
     metas = [meta_buf[j] for j in range(S)]
@@ -362,53 +369,53 @@
     keeps = [jnp.concatenate([m[1:2, :rows]] * F, axis=1) for m in metas]
     coefs = [jnp.concatenate([m[2:3, :rows]] * F, axis=1) for m in metas]
     temb = dot(hot, table_ref[...])
+    side_ref[C : C + 8] = temb
+    side_ref[C + 8 :] = jnp.zeros((32 - C - 8, D), F32)
+    for j in range(S):
+
+        @pl.when(s == j)
+        def _():
+            cut = slice(j * R, (j + 1) * R)
+            side_cut[...] = (side_ref[:, cut] * gain[:, cut]).astype(BF16)
+
+    side_mine = side_cut[...]
+    mix = mix_buf[0].astype(F32)
+    for j in range(1, S):
+        mix = mix + mix_buf[j].astype(F32)
+    mix_lane = lax.broadcasted_iota(jnp.int32, (V, B), 1) // HDIM
+    mix_row = lax.broadcasted_iota(jnp.int32, (V, B), 0) // C
+
+    def late_rows(role, member):
+        turned = dot(wt_ref[member], side_mine, 1, 1)
+        pv_ref[role, :, 2 * rows : 2 * rows + 32] = turned[QK:].astype(BF16)
+        part = jnp.where(member == 0, mix[:, 0:B], mix[:, B : 2 * B])
+        block = jnp.where(
+            mix_lane == mix_row, jnp.concatenate([part] * HZ, axis=0), 0.0
+        )
+        block_hi, block_lo = two(block)
+        values = dot(jnp.concatenate([block_hi, block_lo], axis=0), pv_ref[role])
+        values = values[0:V] + values[V : 2 * V]
+        packs = []
+        for arr in (turned[0:QK], values[:, 2 * rows : 2 * rows + 32]):
+            size = arr.shape[0] // 4
+            packs.append(
+                jnp.concatenate([arr[g * size : (g + 1) * size] for g in range(4)], axis=1)
+            )
+        return jnp.concatenate(
+            [values[:, 0:rows], values[:, rows : 2 * rows]] + packs, axis=0
+        )
+
+    LATE = 2 * V + (QK + V) // 4
+    near_send[2, 0:LATE] = late_rows(1, e_near).astype(BF16)
+    send_near(2, 0, LATE)
+    own_ref[2, 0:LATE] = late_rows(0, e)
     temb_b = temb.astype(BF16)
     ends_buf[f, 2 * C + 8 : 2 * C + 16] = dot(temb_b, pos, 1, 1)
     sides.append(send(ends_buf.at[f], ends_buf.at[f], frame_peer))
     ends_t = dot(ends, temb_b, 1, 1)
     norm_t = jnp.sum(temb * temb, axis=1, keepdims=True)
-    side = jnp.concatenate(
-        [w_in.astype(F32), temb, jnp.zeros((128 - C - 8, D), F32)], axis=0
-    )
-    side_ref[...] = jnp.transpose(side * gain).astype(BF16)
-    side_mine = side_ref[mine]
-    mix = mix_buf[0].astype(F32)
-    for j in range(1, S):
-        mix = mix + mix_buf[j].astype(F32)
-    mix_lane = lax.broadcasted_iota(jnp.int32, (V, B), 1) // HDIM
-    mix_row = lax.broadcasted_iota(jnp.int32, (V, B), 0) // C
-
-    def late_rows(role, member):
-        pv_ref[role, :, 2 * rows : 2 * rows + 128] = dot(
-            wt_ref[member, QK : QK + B], side_mine
-        ).astype(BF16)
-        part = jnp.where(member == 0, mix[:, 0:B], mix[:, B : 2 * B])
-        block = jnp.where(
-            mix_lane == mix_row, jnp.concatenate([part] * HZ, axis=0), 0.0
-        )
-        block_hi, block_lo = two(block)
-        values = dot(jnp.concatenate([block_hi, block_lo], axis=0), pv_ref[role])
-        values = values[0:V] + values[V : 2 * V]
-        turned = dot(wt_ref[member, 0:QK], side_mine)
-        packs = []
-        for arr in (turned, values[:, 2 * rows : 2 * rows + 128]):
-            size = arr.shape[0] // 4
-            packed = arr[0:size]
-            for g in range(1, 4):
-                packed = packed + pltpu.roll(arr[g * size : (g + 1) * size], 32 * g, 1)
-            packs.append(packed)
-        return jnp.concatenate(
-            [values[:, 0:rows], values[:, rows : 2 * rows]] + packs, axis=0
-        )
-
-    LATE = 2 * V + (QK + V) // 4
-    near_send[2, 0:LATE] = late_rows(1, e_near).astype(BF16)
-    tail_rows = pl.ds(0, LATE)
-    near.append(
-        send(near_send.at[2, tail_rows], near_recv.at[2, tail_rows], {"step": s_near})
-    )
-    own_ref[2, 0:LATE] = late_rows(0, e)
-    pass_on(1, 0, QK)
+    for piece in pieces:
+        pass_on(1, *piece)
     pass_on(2, 0, LATE)
 
     scale = 1.4426950408889634 / math.sqrt(HDIM)
@@ -418,7 +425,8 @@
     def whole(i, low, high):
         return far_send[i, low:high].astype(F32) + far_recv[i, low:high].astype(F32)
 
-    far[0].wait_recv()
+    for low, _ in pieces:
+        far[0, low].wait_recv()
     tab_buf[f, 0:QK] = whole(0, 0, QK) * row_scale
     for copy in sides:
         copy.wait_recv()
@@ -436,9 +444,10 @@
             ],
             axis=0,
         )
-    far[1].wait_recv()
+    for low, _ in pieces:
+        far[1, low].wait_recv()
     tab_buf[1 - f, 0:QK] = whole(1, 0, QK) * row_scale
-    far[2].wait_recv()
+    far[2, 0].wait_recv()
     last = whole(2, 0, LATE)
     tab_buf[f, QK : QK + V] = last[0:V]
     tab_buf[1 - f, QK : QK + V] = last[V : 2 * V]
@@ -450,22 +459,21 @@
         jnp.concatenate([ends_in, jnp.zeros((2 * C, 32 - C), F32)], axis=1)
     )
     big = jnp.concatenate(
-        [(big_qk * row_scale).astype(BF16), big_v.astype(BF16), ends_hi, ends_lo], axis=0
+        [ends_hi, ends_lo, (big_qk * row_scale).astype(BF16), big_v.astype(BF16)], axis=0
     )
     tab = jnp.concatenate([tab_buf[i] for i in range(F)], axis=1)
-    T = QK + V
     hot_row = lax.broadcasted_iota(jnp.int32, (32 - C, N), 0)
 
     def partial(x, j):
         xb = x.astype(BF16)
         pick = jnp.where(hot_row == j, 1.0, 0.0).astype(BF16)
         lin = dot(big, jnp.concatenate([xb, pick], axis=0))
-        tail = lin[T : T + 2 * C] + lin[T + 2 * C : T + 4 * C]
+        tail = lin[0 : 2 * C] + lin[2 * C : 4 * C]
         base = base_buf[j]
         square = jnp.sum(xb.astype(F32) * (tail[0:C] + base[0:C]), axis=0, keepdims=True)
         square = jnp.maximum(square + norms[j], 0.0)
         r = lax.rsqrt(square * (1.0 / D) + 1e-06)
-        lin = (lin[0:T] + tab) * r
+        lin = (lin[4 * C :] + tab) * r
         out = jnp.zeros((C, N), F32)
         for n in range(HZ):
             q = lin[n * HDIM : (n + 1) * HDIM].astype(BF16)
@@ -491,18 +499,37 @@
         own = e * PL + q_me
         plane_buf[n, own] = part.astype(BF16)
         slot = plane_buf.at[n, own]
-        flying[key] = [send(slot, slot, group_peer(d)) for d in range(1, 2 * PL)]
+        k = count[0]
+        count[0] += 1
+        for d in range(1, 2 * PL):
+            pltpu.make_async_remote_copy(
+                src_ref=slot,
+                dst_ref=slot,
+                send_sem=ssem.at[k],
+                recv_sem=rsem.at[k],
+                device_id=group_peer(d),
+                device_id_type=MESH,
+            ).start()
+        flying[key] = k
+
+    def settle(n, sem):
+        others = plane_buf.at[n, pl.ds(0, 2 * PL - 1)]
+        pltpu.make_async_copy(others, others, sem).wait()
 
     def land(key):
-        n, j = keys.index(key), key[1]
-        for copy in flying[key]:
-            copy.wait_recv()
+        n, j, k = keys.index(key), key[1], flying[key]
+        settle(n, rsem.at[k])
         total = local_eps[key]
         for i in range(2 * PL):
             total = total + plane_buf[n, i].astype(F32)
         drift[key] = keeps[j] * state[key] + coefs[j] * total
-
-    for act, key in PLAN:
+        settle(n, ssem.at[k])
+
+    for act, key in PLAN[:-1]:
+        if act == "land" and started:
+            for copy in started:
+                copy.wait_send()
+            started.clear()
         {"launch": launch, "land": land}[act](key)
 
     old = [start] * S
@@ -526,6 +553,7 @@
     for it in range(ITERS):
         res = jnp.where(lane == it, norms_out[it], res)
     res_ref[...] = res
+    land(PLAN[-1][1])
     final = jnp.zeros((C, N), F32)
     for j in range(S):
         final = jnp.where(s == j, old[j] + drift[(min(ITERS - 1, j), j)], final)
@@ -533,8 +561,6 @@
     for i in range(1, F):
         half = jnp.where(f == i, final[:, i * rows : (i + 1) * rows], half)
     traj_ref[0] = half
-    for copy in started:
-        copy.wait_send()
 
 
 PLAN = (
@@ -580,7 +606,7 @@
     QK = 2 * B
     V = HZ * C
     n_evals = len(evals_of(S))
-    n_sems = 2 * (S - 1) + 3 + 6 + n_evals * (2 * PL - 1)
+    n_sems = 2 * (S - 1) + 3 + 2 * 7 + n_evals
     vmem = pl.BlockSpec(memory_space=pltpu.VMEM)
     smem = pl.BlockSpec(memory_space=pltpu.SMEM)
     here = pl.BlockSpec(memory_space=pl.ANY)
@@ -602,14 +628,14 @@
             pltpu.VMEM((2, QK + B, R), BF16),
             pltpu.VMEM((D, rows), BF16),
             pltpu.VMEM((R, rows), BF16),
-            pltpu.VMEM((D, 128), BF16),
-            pltpu.VMEM((2, B, N + 128), BF16),
+            pltpu.VMEM((32, D), F32),
+            pltpu.VMEM((32, R), BF16),
+            pltpu.VMEM((2, B, N + 32), BF16),
             pltpu.VMEM((3, QK, rows), F32),
             pltpu.VMEM((3, QK, rows), BF16),
             pltpu.VMEM((3, QK, rows), BF16),
             pltpu.VMEM((3, QK, rows), BF16),
             pltpu.VMEM((3, QK, rows), BF16),
-            pltpu.VMEM((C, 2 * B), BF16),
             pltpu.VMEM((S, C, 2 * B), BF16),
             pltpu.VMEM((F, C, rows), F32),
             pltpu.VMEM((S, 8, time_table.shape[0]), F32),

time: 41.1 us -> 39.6 us (0.964)
  Pallas kernels: 37.8 us -> 36.3 us
    pallas_call x1, Pallas kernels: 37.8 us -> 36.3 us  [local_heads(): pl.pallas_call(functools.partial(kernel, S, F, H), out_shape=(pltpu.VMEM(...]
where the time goes in v2:
time: 39.6 us; the launch traced here: 39.4 us
  Pallas kernels  36.3 us (92%)
  between operations  1.93 us (5%)
  local copies, waits for them, and re-layouts  1.11 us (3%)
    pallas_call x1, Pallas kernels, local_heads(): pl.pallas_call(functools.partial(kernel, S, F, H), out_shape=(pltpu.VMEM(...  36.3 us
    unnamed x2, local copies, waits for them, and re-layouts  1.11 us

profile of v2, /device:TPU:0, one launch (start us, length us, event | category | flops | bytes accessed | tf_op | source)
XLA Modules:
  0.0 39.4 jit_solution(11438938882251069997)
XLA Ops:
  1.9 36.3 %shard_map.131 = (f32[1,16,128]{2,1,0:T(8,128)S(1)}, f32[1,4]{1,0:T(1,128)S(1)}) custom-call(f32[16,128]{1,0:T(8,128)} %noise_hbm.1, bf16[128,1152]{1,0:T(8,128)(2,1)} %pos_hbm.1, bf16[128,1152]{1,0:T(8,128)(2,1)} %table_hbm.1, s32[1]{0:T(128)S(6)} %copy.18.tidx_ref, s32[1]{0:T(128)S(6)} %copy.19.sidx_ref, f32[1,128]{1,0:T(1,128)} %bitcast.6, ...), custom_call_target="tpu_custom_call" | custom-call | tf_op jit(solution)/shard_map/pallas_call | solution.py:613
  38.3 0.6 %copy.16 = f32[1,16,128]{2,1,0:T(8,128)} copy(f32[1,16,128]{2,1,0:T(8,128)S(1)} %get-tuple-element.6) | data formatting | bytes 16384
  38.9 0.5 %copy.17 = f32[4]{0:T(128)} copy(f32[4]{0:T(128)S(1)} %bitcast.4) | data formatting | bytes 32

commit v3 on v2

--- a/solution.py
+++ b/solution.py
@@ -148,12 +148,6 @@
     return high, (a - high.astype(F32)).astype(BF16)
 
 
-def evals_of(steps):
-    return [(i, j) for j in range(steps - 1) for i in range(min(j, ITERS - 1) + 1)] + [
-        (min(ITERS, steps) - 1, steps - 1)
-    ]
-
-
 def kernel(
     S,
     F,
@@ -196,9 +190,13 @@
     noise_buf,
     meta_buf,
     ends_buf,
+    fin_qk,
+    fin_late,
+    big_buf,
     tab_buf,
     base_buf,
     plane_buf,
+    chip_buf,
     ssem,
     rsem,
 ):
@@ -242,9 +240,12 @@
         return {"step": lax.rem(s + d, S)}
 
     def group_peer(d):
-        t = lax.rem(q_me + lax.rem(d, PL), PL)
-        z = s_near if d >= PL else s
-        return {"step": z, "frame": t // H, "head": lax.rem(t, H)}
+        dz, df, dh = d // PL, d % PL // H, d % H
+        return {
+            "step": s_near if dz else s,
+            "frame": lax.rem(f + df, F),
+            "head": lax.rem(h + dh, H),
+        }
 
     frame_peer = {"frame": 1 - f}
 
@@ -286,15 +287,18 @@
     gain = gain_ref[...].reshape(1, D)
     pos = pos_ref[...]
     at_ref[...] = jnp.transpose(pos.astype(F32) * gain).astype(BF16)
-    for i in range(F):
-
-        @pl.when(f == i)
-        def _():
-            for p in range(3):
-                turned = jnp.transpose(wqkv_ref[p, :, i * 2 * B : (i + 1) * 2 * B])
-                for t in range(2):
-                    wt_ref[t, p * B : (p + 1) * B] = turned[t * B : (t + 1) * B]
-
+
+    def turn_weights(parts):
+        for i in range(F):
+
+            @pl.when(f == i)
+            def _():
+                for p in parts:
+                    turned = jnp.transpose(wqkv_ref[p, :, i * 2 * B : (i + 1) * 2 * B])
+                    for t in range(2):
+                        wt_ref[t, p * B : (p + 1) * B] = turned[t * B : (t + 1) * B]
+
+    turn_weights((0, 1))
     mine = pl.ds(pl.multiple_of(s * R, R), R)
     at_mine = at_ref[mine]
     near_send[0] = dot(wt_ref[e_near, 0:QK], at_mine).astype(BF16)
@@ -327,6 +331,7 @@
     loads[7].wait()
     sides = [send(noise_buf.at[f], noise_buf.at[f], frame_peer)]
     own_ref[0] = dot(wt_ref[e, 0:QK], at_mine)
+    turn_weights((2,))
 
     def pass_on(i, low, high):
         near[i, low].wait_recv()
@@ -416,18 +421,50 @@
     norm_t = jnp.sum(temb * temb, axis=1, keepdims=True)
     for piece in pieces:
         pass_on(1, *piece)
-    pass_on(2, 0, LATE)
 
     scale = 1.4426950408889634 / math.sqrt(HDIM)
     qk_row = lax.broadcasted_iota(jnp.int32, (QK, 1), 0)
     row_scale = jnp.where(qk_row < B, scale, 1.0)
+    set_own, set_near = 2 * f + e, 2 * f + e_near
+    halves = (f, 1 - f)
 
     def whole(i, low, high):
-        return far_send[i, low:high].astype(F32) + far_recv[i, low:high].astype(F32)
-
-    for low, _ in pieces:
-        far[0, low].wait_recv()
-    tab_buf[f, 0:QK] = whole(0, 0, QK) * row_scale
+        far[i, low].wait_recv()
+        total = far_send[i, low:high].astype(F32) + far_recv[i, low:high].astype(F32)
+        return total.astype(BF16)
+
+    def finish(i, low, high):
+        total = whole(i, low, high)
+        window = pl.ds(low, high - low)
+        if i < 2:
+            fin_qk[set_own, halves[i], low:high] = total
+            ref = fin_qk.at[set_own, halves[i], window]
+            twin = fin_qk.at[set_near, halves[i], window]
+        else:
+            fin_late[set_own] = total
+            ref = fin_late.at[set_own]
+            twin = fin_late.at[set_near]
+        return ref, twin
+
+    across, shared, passed = [], [], []
+
+    def cross_over(refs):
+        across.append(send(refs[0], refs[0], frame_peer))
+
+    def share(refs):
+        shared.append((send(refs[0], refs[0], to_near), refs[1]))
+
+    def forward(number):
+        for _ in range(number):
+            copy, twin = shared.pop(0)
+            copy.wait_recv()
+            passed.append(send(twin, twin, frame_peer))
+
+    ready = [finish(0, *piece) for piece in pieces]
+    pass_on(2, 0, LATE)
+    for refs in ready:
+        cross_over(refs)
+        share(refs)
     for copy in sides:
         copy.wait_recv()
     start = jnp.concatenate([noise_buf[i] for i in range(F)], axis=1)
@@ -444,119 +481,187 @@
             ],
             axis=0,
         )
-    for low, _ in pieces:
-        far[1, low].wait_recv()
-    tab_buf[1 - f, 0:QK] = whole(1, 0, QK) * row_scale
-    far[2, 0].wait_recv()
-    last = whole(2, 0, LATE)
-    tab_buf[f, QK : QK + V] = last[0:V]
-    tab_buf[1 - f, QK : QK + V] = last[V : 2 * V]
-    packed = last[2 * V : LATE]
-    size = QK // 4
-    big_qk = jnp.concatenate([packed[0:size, 32 * g : 32 * g + 32] for g in range(4)], axis=0)
-    big_v = jnp.concatenate([packed[size:, 32 * g : 32 * g + 32] for g in range(4)], axis=0)
     ends_hi, ends_lo = two(
         jnp.concatenate([ends_in, jnp.zeros((2 * C, 32 - C), F32)], axis=1)
     )
-    big = jnp.concatenate(
-        [ends_hi, ends_lo, (big_qk * row_scale).astype(BF16), big_v.astype(BF16)], axis=0
-    )
-    tab = jnp.concatenate([tab_buf[i] for i in range(F)], axis=1)
+    ends_big = jnp.concatenate([ends_hi, ends_lo], axis=0)
+    size = QK // 4
+
+    def build(slot, group, frame):
+        last = fin_late[group].astype(F32)
+        one, other = last[0:V], last[V : 2 * V]
+        packed = last[2 * V : LATE]
+        big_qk = jnp.concatenate(
+            [packed[0:size, 32 * g : 32 * g + 32] for g in range(4)], axis=0
+        )
+        big_v = jnp.concatenate(
+            [packed[size:, 32 * g : 32 * g + 32] for g in range(4)], axis=0
+        )
+        big_buf[slot, 0:QK] = (big_qk * row_scale).astype(BF16)
+        big_buf[slot, QK:] = big_v.astype(BF16)
+        for i in range(F):
+            cut = slice(i * rows, (i + 1) * rows)
+            tab_buf[slot, 0:QK, cut] = fin_qk[group, i].astype(F32) * row_scale
+            tab_buf[slot, QK:, cut] = jnp.where(frame == i, one, other)
+
+    ready = [finish(1, *piece) for piece in pieces]
+    for refs in ready:
+        cross_over(refs)
+        share(refs)
+    ready = finish(2, 0, LATE)
+    build(4, set_own, f)
+
+    def share_rest(_):
+        cross_over(ready)
+        share(ready)
+
     hot_row = lax.broadcasted_iota(jnp.int32, (32 - C, N), 0)
-
-    def partial(x, j):
+    ones_rows = jnp.ones((C, N), BF16)
+
+    def evaluate(x, j, slots):
         xb = x.astype(BF16)
         pick = jnp.where(hot_row == j, 1.0, 0.0).astype(BF16)
-        lin = dot(big, jnp.concatenate([xb, pick], axis=0))
-        tail = lin[0 : 2 * C] + lin[2 * C : 4 * C]
+        x_in = jnp.concatenate([xb, pick], axis=0)
         base = base_buf[j]
-        square = jnp.sum(xb.astype(F32) * (tail[0:C] + base[0:C]), axis=0, keepdims=True)
-        square = jnp.maximum(square + norms[j], 0.0)
-        r = lax.rsqrt(square * (1.0 / D) + 1e-06)
-        lin = (lin[4 * C :] + tab) * r
         out = jnp.zeros((C, N), F32)
-        for n in range(HZ):
-            q = lin[n * HDIM : (n + 1) * HDIM].astype(BF16)
-            k = lin[B + n * HDIM : B + (n + 1) * HDIM].astype(BF16)
-            v_hi, v_lo = two(lin[QK + n * C : QK + (n + 1) * C])
-            scores = dot(k, q, 0, 0)
-            p = jnp.exp2(scores - jnp.max(scores, axis=0, keepdims=True)).astype(BF16)
-            o = dot(jnp.concatenate([v_hi, v_lo, jnp.ones((C, N), BF16)], axis=0), p)
-            out = out + (o[0:C] + o[C : 2 * C]) / o[2 * C : 2 * C + 1]
-        return out, tail[C : 2 * C] + base[C : 2 * C]
-
-    keys = evals_of(S)
+        items, scores, r, eps = {}, {}, None, None
+        G = len(slots)
+        for g in range(G + 2):
+            if g < G:
+                big = big_buf[slots[g]]
+                if g == 0:
+                    lin = dot(jnp.concatenate([ends_big, big], axis=0), x_in)
+                    tail = lin[0 : 2 * C] + lin[2 * C : 4 * C]
+                    lin = lin[4 * C :]
+                    square = jnp.sum(
+                        xb.astype(F32) * (tail[0:C] + base[0:C]), axis=0, keepdims=True
+                    )
+                    square = jnp.maximum(square + norms[j], 0.0)
+                    r = lax.rsqrt(square * (1.0 / D) + 1e-06)
+                    eps = tail[C : 2 * C] + base[C : 2 * C]
+                else:
+                    lin = dot(big, x_in)
+                lin = (lin + tab_buf[slots[g]]) * r
+                for n in range(HZ):
+                    q = lin[n * HDIM : (n + 1) * HDIM].astype(BF16)
+                    k = lin[B + n * HDIM : B + (n + 1) * HDIM].astype(BF16)
+                    v_hi, v_lo = two(lin[QK + n * C : QK + (n + 1) * C])
+                    items[g, n] = q, k, jnp.concatenate([v_hi, v_lo, ones_rows], axis=0)
+            if 0 <= g - 1 < G:
+                for n in range(HZ):
+                    q, k, _ = items[g - 1, n]
+                    scores[g - 1, n] = dot(k, q, 0, 0)
+            if 0 <= g - 2 < G:
+                for n in range(HZ):
+                    block = scores.pop((g - 2, n))
+                    top = jnp.max(block, axis=0, keepdims=True)
+                    p = jnp.exp2(block - top).astype(BF16)
+                    o = dot(items[g - 2, n][2], p)
+                    out = out + (o[0:C] + o[C : 2 * C]) / o[2 * C : 2 * C + 1]
+        return out, eps
+
+    spread = [key for act, key in PLAN if act == "spread"]
+    local = [key for act, key in PLAN if act == "local"]
     state, local_eps, drift, flying = {}, {}, {}, {}
-
-    def launch(key):
+    outward = sorted(
+        range(1, 2 * PL), key=lambda d: (-(d // PL + (d % PL // H > 0)), -(d // PL))
+    )
+
+    def launch(key, slots):
         i, j = key
-        n = keys.index(key)
         x = start
         for m in range(j if i else 0):
             x = x + drift[(min(i - 1, m), m)]
         state[key] = x
-        part, local_eps[key] = partial(x, j)
-        own = e * PL + q_me
-        plane_buf[n, own] = part.astype(BF16)
-        slot = plane_buf.at[n, own]
+        part, local_eps[key] = evaluate(x, j, slots)
         k = count[0]
         count[0] += 1
-        for d in range(1, 2 * PL):
+        if key in spread:
+            slot = plane_buf.at[spread.index(key), e * PL + q_me]
+            slot[...] = part.astype(BF16)
+            peers = [group_peer(d) for d in outward]
+        else:
+            slot = chip_buf.at[local.index(key), h]
+            slot[...] = part
+            peers = [{"head": 1 - h}]
+        for peer in peers:
             pltpu.make_async_remote_copy(
                 src_ref=slot,
                 dst_ref=slot,
                 send_sem=ssem.at[k],
                 recv_sem=rsem.at[k],
-                device_id=group_peer(d),
+                device_id=peer,
                 device_id_type=MESH,
             ).start()
         flying[key] = k
 
-    def settle(n, sem):
-        others = plane_buf.at[n, pl.ds(0, 2 * PL - 1)]
+    def settle(key, sem):
+        if key in spread:
+            others = plane_buf.at[spread.index(key), pl.ds(0, 2 * PL - 1)]
+        else:
+            others = chip_buf.at[local.index(key), 0]
         pltpu.make_async_copy(others, others, sem).wait()
 
     def land(key):
-        n, j, k = keys.index(key), key[1], flying[key]
-        settle(n, rsem.at[k])
+        j, k = key[1], flying[key]
+        settle(key, rsem.at[k])
         total = local_eps[key]
-        for i in range(2 * PL):
-            total = total + plane_buf[n, i].astype(F32)
+        if key in spread:
+            for i in range(2 * PL):
+                total = total + plane_buf[spread.index(key), i].astype(F32)
+        else:
+            for i in range(H):
+                total = total + chip_buf[local.index(key), i]
         drift[key] = keeps[j] * state[key] + coefs[j] * total
-        settle(n, ssem.at[k])
-
-    for act, key in PLAN[:-1]:
-        if act == "land" and started:
-            for copy in started:
-                copy.wait_send()
-            started.clear()
-        {"launch": launch, "land": land}[act](key)
-
-    old = [start] * S
-    norms_out = []
-    for it in range(ITERS):
-        new, run = [], start
-        for j in range(S):
-            new.append(run)
-            if j < S - 1:
-                run = run + drift[(min(it, j), j)]
-        square = jnp.zeros((1, 1), F32)
-        for j in range(S):
-            change = new[j] - old[j]
-            square = square + jnp.sum(
-                jnp.sum(change * change, axis=0, keepdims=True), axis=1, keepdims=True
+        settle(key, ssem.at[k])
+
+    def clear(_):
+        for copy in started:
+            copy.wait_send()
+        started.clear()
+
+    def gather(_):
+        for copy in across + passed:
+            copy.wait_recv()
+        for g in range(2 * F):
+            build(g, g, g // 2)
+
+    def norms_now(_):
+        lane = lax.broadcasted_iota(jnp.int32, res_ref.shape, 1)
+        res = jnp.zeros(res_ref.shape, F32)
+        old = [start] * S
+        for it in range(ITERS):
+            new, run = [], start
+            for j in range(S):
+                new.append(run)
+                if j < S - 1:
+                    run = run + drift[(min(it, j), j)]
+            square = jnp.zeros((C, N), F32)
+            for j in range(1, S):
+                change = new[j] - old[j]
+                square = square + change * change
+            square = jnp.sum(
+                jnp.sum(square, axis=0, keepdims=True), axis=1, keepdims=True
             )
-        norms_out.append(jnp.sqrt(square / (S * C * N) + 1e-06))
-        old = new
-    lane = lax.broadcasted_iota(jnp.int32, res_ref.shape, 1)
-    res = jnp.zeros(res_ref.shape, F32)
-    for it in range(ITERS):
-        res = jnp.where(lane == it, norms_out[it], res)
-    res_ref[...] = res
-    land(PLAN[-1][1])
+            res = jnp.where(lane == it, jnp.sqrt(square / (S * C * N) + 1e-06), res)
+            old = new
+        res_ref[...] = res
+
+    acts = {
+        "clear": clear,
+        "share": share_rest,
+        "forward": forward,
+        "gather": gather,
+        "land": land,
+        "norms": norms_now,
+        "spread": lambda key: launch(key, [2 * F]),
+        "local": lambda key: launch(key, list(range(2 * F))),
+    }
+    for act, key in PLAN:
+        acts[act](key)
     final = jnp.zeros((C, N), F32)
     for j in range(S):
-        final = jnp.where(s == j, old[j] + drift[(min(ITERS - 1, j), j)], final)
+        final = jnp.where(s == j, state[(j, j)] + drift[(j, j)], final)
     half = final[:, 0:rows]
     for i in range(1, F):
         half = jnp.where(f == i, final[:, i * rows : (i + 1) * rows], half)
@@ -564,19 +669,25 @@
 
 
 PLAN = (
-    ("launch", (0, 0)),
-    ("launch", (0, 1)),
-    ("launch", (0, 2)),
+    ("spread", (0, 0)),
+    ("share", None),
+    ("forward", 6),
+    ("spread", (0, 1)),
     ("land", (0, 0)),
-    ("launch", (1, 1)),
+    ("spread", (1, 1)),
+    ("forward", 1),
     ("land", (0, 1)),
-    ("launch", (1, 2)),
+    ("spread", (0, 2)),
+    ("spread", (1, 2)),
+    ("gather", None),
+    ("clear", None),
     ("land", (1, 1)),
-    ("launch", (2, 2)),
+    ("local", (2, 2)),
+    ("land", (2, 2)),
+    ("local", (3, 3)),
     ("land", (0, 2)),
     ("land", (1, 2)),
-    ("land", (2, 2)),
-    ("launch", (3, 3)),
+    ("norms", None),
     ("land", (3, 3)),
 )
 
@@ -605,8 +716,10 @@
     B = HZ * HDIM
     QK = 2 * B
     V = HZ * C
-    n_evals = len(evals_of(S))
-    n_sems = 2 * (S - 1) + 3 + 2 * 7 + n_evals
+    late = 2 * V + (QK + V) // 4
+    n_spread = sum(act == "spread" for act, _ in PLAN)
+    n_local = sum(act == "local" for act, _ in PLAN)
+    n_sems = 2 * (S - 1) + 3 + 5 * 7 + n_spread + n_local
     vmem = pl.BlockSpec(memory_space=pltpu.VMEM)
     smem = pl.BlockSpec(memory_space=pltpu.SMEM)
     here = pl.BlockSpec(memory_space=pl.ANY)
@@ -640,9 +753,13 @@
             pltpu.VMEM((F, C, rows), F32),
             pltpu.VMEM((S, 8, time_table.shape[0]), F32),
             pltpu.VMEM((F, 2 * C + 16, rows), F32),
-            pltpu.VMEM((F, QK + V, rows), F32),
+            pltpu.VMEM((2 * F, F, QK, rows), BF16),
+            pltpu.VMEM((2 * F, late, rows), BF16),
+            pltpu.VMEM((2 * F + 1, QK + V, 32), BF16),
+            pltpu.VMEM((2 * F + 1, QK + V, N), F32),
             pltpu.VMEM((S, 2 * C, N), F32),
-            pltpu.VMEM((n_evals, 2 * PL, C, N), BF16),
+            pltpu.VMEM((n_spread, 2 * PL, C, N), BF16),
+            pltpu.VMEM((n_local, H, C, N), F32),
             pltpu.SemaphoreType.DMA((n_sems + 10,)),
             pltpu.SemaphoreType.DMA((n_sems,)),
         ],

time: 39.6 us -> 36.8 us (0.929)
  Pallas kernels: 36.3 us -> 33.6 us
    pallas_call x1, Pallas kernels: 36.3 us -> 33.6 us  [local_heads(): pl.pallas_call(functools.partial(kernel, S, F, H), out_shape=(pltpu.VMEM(...]
where the time goes in v3:
time: 36.8 us; the launch traced here: 36.6 us
  Pallas kernels  33.6 us (91%)
  between operations  1.93 us (5%)
  local copies, waits for them, and re-layouts  1.11 us (3%)
    pallas_call x1, Pallas kernels, local_heads(): pl.pallas_call(functools.partial(kernel, S, F, H), out_shape=(pltpu.VMEM(...  33.6 us
    unnamed x2, local copies, waits for them, and re-layouts  1.11 us

profile of v3, /device:TPU:0, one launch (start us, length us, event | category | flops | bytes accessed | tf_op | source)
XLA Modules:
  0.0 36.6 jit_solution(4530470970666542800)
XLA Ops:
  1.9 33.6 %shard_map.131 = (f32[1,16,128]{2,1,0:T(8,128)S(1)}, f32[1,4]{1,0:T(1,128)S(1)}) custom-call(f32[16,128]{1,0:T(8,128)} %noise_hbm.1, bf16[128,1152]{1,0:T(8,128)(2,1)} %pos_hbm.1, bf16[128,1152]{1,0:T(8,128)(2,1)} %table_hbm.1, s32[1]{0:T(128)S(6)} %copy.18.tidx_ref, s32[1]{0:T(128)S(6)} %copy.19.sidx_ref, f32[1,128]{1,0:T(1,128)} %bitcast.6, ...), custom_call_target="tpu_custom_call" | custom-call | tf_op jit(solution)/shard_map/pallas_call | solution.py:726
  35.5 0.6 %copy.16 = f32[1,16,128]{2,1,0:T(8,128)} copy(f32[1,16,128]{2,1,0:T(8,128)S(1)} %get-tuple-element.6) | data formatting | bytes 16384
  36.1 0.5 %copy.17 = f32[4]{0:T(128)} copy(f32[4]{0:T(128)S(1)} %bitcast.4) | data formatting | bytes 32

commit v4 on v3

--- a/solution.py
+++ b/solution.py
@@ -209,7 +209,9 @@
                 (coef_hbm, coef_ref),
                 (gain_hbm, gain_ref),
                 (pos_hbm, pos_ref),
-                (wqkv_hbm, wqkv_ref),
+                (wqkv_hbm.at[0], wqkv_ref.at[0]),
+                (wqkv_hbm.at[1], wqkv_ref.at[1]),
+                (wqkv_hbm.at[2], wqkv_ref.at[2]),
                 (wfin_hbm, wfin_ref),
                 (wproj_hbm, wproj_ref),
                 (noise_hbm, noise_buf.at[f]),
@@ -282,8 +284,7 @@
     keep = jnp.sum(jnp.where(hot_s, keep_ref[...], 0.0), axis=1, keepdims=True)
     coef = jnp.sum(jnp.where(hot_s, coef_ref[...], 0.0), axis=1, keepdims=True)
     meta_buf[s] = jnp.where(row_id == 0, hot_t, jnp.where(row_id == 1, keep, coef))
-    for copy in loads[3:5]:
-        copy.wait()
+    loads[3].wait()
     gain = gain_ref[...].reshape(1, D)
     pos = pos_ref[...]
     at_ref[...] = jnp.transpose(pos.astype(F32) * gain).astype(BF16)
@@ -298,6 +299,8 @@
                     for t in range(2):
                         wt_ref[t, p * B : (p + 1) * B] = turned[t * B : (t + 1) * B]
 
+    for p in range(2):
+        loads[4 + p].wait()
     turn_weights((0, 1))
     mine = pl.ds(pl.multiple_of(s * R, R), R)
     at_mine = at_ref[mine]
@@ -317,7 +320,7 @@
     turn = send(at_ref.at[mine], at_peer, frame_peer)
     for piece in pieces[1:]:
         send_near(0, *piece)
-    for copy in loads[5:7]:
+    for copy in loads[7:9]:
         copy.wait()
     rows_of = wfin_ref[:, 0:R].astype(F32)
     for j in range(1, S):
@@ -328,9 +331,10 @@
         picked = jnp.where(f == i, folded[:, i * 2 * B : (i + 1) * 2 * B], picked)
     mix_buf[s] = picked.astype(BF16)
     early += [send(mix_buf.at[s], mix_buf.at[s], step_peer(d)) for d in order]
-    loads[7].wait()
+    loads[9].wait()
     sides = [send(noise_buf.at[f], noise_buf.at[f], frame_peer)]
     own_ref[0] = dot(wt_ref[e, 0:QK], at_mine)
+    loads[6].wait()
     turn_weights((2,))
 
     def pass_on(i, low, high):
@@ -340,11 +344,9 @@
         window = pl.ds(low, high - low)
         far[i, low] = send(far_send.at[i, window], far_recv.at[i, window], to_far)
 
-    for piece in pieces:
-        pass_on(0, *piece)
     pv_ref[0, :, 0:rows] = dot(wt_ref[e, QK : QK + B], at_mine).astype(BF16)
     pv_ref[1, :, 0:rows] = dot(wt_ref[e_near, QK : QK + B], at_mine).astype(BF16)
-    for copy in loads[8:]:
+    for copy in loads[10:]:
         copy.wait()
     w_in = win_ref[...]
     ends = jnp.concatenate([w_in, wfin_ref[...]], axis=0)
@@ -355,6 +357,8 @@
     ends_buf[f, 0 : 2 * C] = dot(ends, pos, 1, 1)
     ends_buf[f, 2 * C : 2 * C + 8] = dot(ones, sq_hi, 1, 1) + dot(ones, sq_lo, 1, 1)
 
+    for piece in pieces:
+        pass_on(0, *piece)
     turn.wait_recv()
     at_other = at_peer[...]
     near_send[1] = dot(wt_ref[e_near, 0:QK], at_other).astype(BF16)
@@ -621,10 +625,13 @@
         started.clear()
 
     def gather(_):
-        for copy in across + passed:
-            copy.wait_recv()
-        for g in range(2 * F):
-            build(g, g, g // 2)
+        build(set_own, set_own, f)
+        build(set_near, set_near, f)
+        for copies, member in ((across, e), (passed, e_near)):
+            for copy in copies:
+                copy.wait_recv()
+            twin = 2 * (1 - f) + member
+            build(twin, twin, 1 - f)
 
     def norms_now(_):
         lane = lax.broadcasted_iota(jnp.int32, res_ref.shape, 1)
@@ -669,13 +676,13 @@
 
 
 PLAN = (
+    ("share", None),
     ("spread", (0, 0)),
-    ("share", None),
     ("forward", 6),
     ("spread", (0, 1)),
     ("land", (0, 0)),
+    ("forward", 1),
     ("spread", (1, 1)),
-    ("forward", 1),
     ("land", (0, 1)),
     ("spread", (0, 2)),
     ("spread", (1, 2)),
@@ -760,7 +767,7 @@
             pltpu.VMEM((S, 2 * C, N), F32),
             pltpu.VMEM((n_spread, 2 * PL, C, N), BF16),
             pltpu.VMEM((n_local, H, C, N), F32),
-            pltpu.SemaphoreType.DMA((n_sems + 10,)),
+            pltpu.SemaphoreType.DMA((n_sems + 12,)),
             pltpu.SemaphoreType.DMA((n_sems,)),
         ],
         compiler_params=pltpu.CompilerParams(

time: 36.8 us -> 35.6 us (0.967)
  Pallas kernels: 33.6 us -> 32.4 us
    pallas_call x1, Pallas kernels: 33.6 us -> 32.4 us  [local_heads(): pl.pallas_call(functools.partial(kernel, S, F, H), out_shape=(pltpu.VMEM(...]
where the time goes in v4:
time: 35.6 us; the launch traced here: 35.5 us
  Pallas kernels  32.4 us (91%)
  between operations  1.93 us (5%)
  local copies, waits for them, and re-layouts  1.11 us (3%)
    pallas_call x1, Pallas kernels, local_heads(): pl.pallas_call(functools.partial(kernel, S, F, H), out_shape=(pltpu.VMEM(...  32.4 us
    unnamed x2, local copies, waits for them, and re-layouts  1.11 us

profile of v4, /device:TPU:0, one launch (start us, length us, event | category | flops | bytes accessed | tf_op | source)
XLA Modules:
  0.0 35.5 jit_solution(17825608487391823270)
XLA Ops:
  1.9 32.4 %shard_map.131 = (f32[1,16,128]{2,1,0:T(8,128)S(1)}, f32[1,4]{1,0:T(1,128)S(1)}) custom-call(f32[16,128]{1,0:T(8,128)} %noise_hbm.1, bf16[128,1152]{1,0:T(8,128)(2,1)} %pos_hbm.1, bf16[128,1152]{1,0:T(8,128)(2,1)} %table_hbm.1, s32[1]{0:T(128)S(6)} %copy.18.tidx_ref, s32[1]{0:T(128)S(6)} %copy.19.sidx_ref, f32[1,128]{1,0:T(1,128)} %bitcast.6, ...), custom_call_target="tpu_custom_call" | custom-call | tf_op jit(solution)/shard_map/pallas_call | solution.py:733
  34.3 0.6 %copy.16 = f32[1,16,128]{2,1,0:T(8,128)} copy(f32[1,16,128]{2,1,0:T(8,128)S(1)} %get-tuple-element.6) | data formatting | bytes 16384
  34.9 0.5 %copy.17 = f32[4]{0:T(128)} copy(f32[4]{0:T(128)S(1)} %bitcast.4) | data formatting | bytes 32

commit v5 on v4

--- a/solution.py
+++ b/solution.py
@@ -202,7 +202,7 @@
 ):
     s, f, h = (lax.axis_index(a) for a in ("step", "frame", "head"))
     loads = [
-        pltpu.make_async_copy(src, dst, ssem.at[ssem.shape[0] - 1 - n])
+        pltpu.make_async_copy(src, dst, ssem.at[n])
         for n, (src, dst) in enumerate(
             (
                 (keep_hbm, keep_ref),
@@ -257,23 +257,34 @@
     for d in range(1, S):
         pl.semaphore_signal(barrier, inc=1, device_id=step_peer(d), device_id_type=MESH)
 
-    count = [0]
-    started = []
-
-    def send(src, dst, peer):
-        k = count[0]
-        count[0] += 1
-        copy = pltpu.make_async_remote_copy(
+    reused = ("across", "share", "pass", "late", "pass late", "ends")
+    fresh = ("near", "far", "turn", "meta", "mix", "noise")
+    outs = {name: n for n, name in enumerate(reused)}
+    outs.update((name, len(loads) + n) for n, name in enumerate(fresh))
+    spare = list(range(len(reused), len(loads)))
+    spare += list(range(len(loads) + len(fresh), ssem.shape[0]))
+    ins = {}
+
+    def prepare(src, dst, peer, out, into):
+        return pltpu.make_async_remote_copy(
             src_ref=src,
             dst_ref=dst,
-            send_sem=ssem.at[k],
-            recv_sem=rsem.at[k],
+            send_sem=ssem.at[outs[out]],
+            recv_sem=rsem.at[ins.setdefault(into, len(ins))],
             device_id=peer,
             device_id_type=MESH,
         )
+
+    def send(src, dst, peer, out, into):
+        copy = prepare(src, dst, peer, out, into)
         copy.start()
-        started.append(copy)
         return copy
+
+    def settle(ref, sem):
+        pltpu.make_async_copy(ref, ref, sem).wait()
+
+    def arrive(ref, into):
+        settle(ref, rsem.at[ins[into]])
 
     for copy in loads[:3]:
         copy.wait()
@@ -311,13 +322,20 @@
 
     def send_near(i, low, high):
         window = pl.ds(low, high - low)
-        near[i, low] = send(near_send.at[i, window], near_recv.at[i, window], to_near)
+        near[i, low] = send(
+            near_send.at[i, window],
+            near_recv.at[i, window],
+            to_near,
+            "late" if i == 2 else "near",
+            ("near", i, low),
+        )
 
     pieces = [(low, low + QK // 3) for low in range(0, QK, QK // 3)]
     order = sorted(range(1, S), key=lambda d: abs(d - S / 2))
-    early = [send(meta_buf.at[s], meta_buf.at[s], step_peer(d)) for d in order]
+    for d in order:
+        send(meta_buf.at[s], meta_buf.at[s], step_peer(d), "meta", "meta")
     send_near(0, *pieces[0])
-    turn = send(at_ref.at[mine], at_peer, frame_peer)
+    turn = send(at_ref.at[mine], at_peer, frame_peer, "turn", "turn")
     for piece in pieces[1:]:
         send_near(0, *piece)
     for copy in loads[7:9]:
@@ -330,9 +348,10 @@
     for i in range(1, F):
         picked = jnp.where(f == i, folded[:, i * 2 * B : (i + 1) * 2 * B], picked)
     mix_buf[s] = picked.astype(BF16)
-    early += [send(mix_buf.at[s], mix_buf.at[s], step_peer(d)) for d in order]
+    for d in order:
+        send(mix_buf.at[s], mix_buf.at[s], step_peer(d), "mix", "mix")
     loads[9].wait()
-    sides = [send(noise_buf.at[f], noise_buf.at[f], frame_peer)]
+    sides = [send(noise_buf.at[f], noise_buf.at[f], frame_peer, "noise", "noise")]
     own_ref[0] = dot(wt_ref[e, 0:QK], at_mine)
     loads[6].wait()
     turn_weights((2,))
@@ -342,7 +361,13 @@
         total = own_ref[i, low:high] + near_recv[i, low:high].astype(F32)
         far_send[i, low:high] = total.astype(BF16)
         window = pl.ds(low, high - low)
-        far[i, low] = send(far_send.at[i, window], far_recv.at[i, window], to_far)
+        far[i, low] = send(
+            far_send.at[i, window],
+            far_recv.at[i, window],
+            to_far,
+            "late" if i == 2 else "far",
+            ("far", i, low),
+        )
 
     pv_ref[0, :, 0:rows] = dot(wt_ref[e, QK : QK + B], at_mine).astype(BF16)
     pv_ref[1, :, 0:rows] = dot(wt_ref[e_near, QK : QK + B], at_mine).astype(BF16)
@@ -369,8 +394,8 @@
     pv_ref[1, :, rows : 2 * rows] = dot(wt_ref[e_near, QK : QK + B], at_other).astype(BF16)
 
     side_ref[0:C] = w_in.astype(F32)
-    for copy in early:
-        copy.wait_recv()
+    arrive(meta_buf.at[pl.ds(0, S - 1)], "meta")
+    arrive(mix_buf.at[pl.ds(0, S - 1)], "mix")
     metas = [meta_buf[j] for j in range(S)]
     hot = jnp.concatenate(
         [m[0:1] for m in metas] + [jnp.zeros((8 - S, lanes), F32)], axis=0
@@ -420,7 +445,7 @@
     own_ref[2, 0:LATE] = late_rows(0, e)
     temb_b = temb.astype(BF16)
     ends_buf[f, 2 * C + 8 : 2 * C + 16] = dot(temb_b, pos, 1, 1)
-    sides.append(send(ends_buf.at[f], ends_buf.at[f], frame_peer))
+    sides.append(send(ends_buf.at[f], ends_buf.at[f], frame_peer, "ends", "ends"))
     ends_t = dot(ends, temb_b, 1, 1)
     norm_t = jnp.sum(temb * temb, axis=1, keepdims=True)
     for piece in pieces:
@@ -450,25 +475,34 @@
             twin = fin_late.at[set_near]
         return ref, twin
 
-    across, shared, passed = [], [], []
-
-    def cross_over(refs):
-        across.append(send(refs[0], refs[0], frame_peer))
-
-    def share(refs):
-        shared.append((send(refs[0], refs[0], to_near), refs[1]))
-
-    def forward(number):
-        for _ in range(number):
-            copy, twin = shared.pop(0)
+    shared = []
+
+    def hand_on(refs, kind):
+        send(refs[0], refs[0], frame_peer, kind or "across", kind and "late" or "across")
+
+    def share(refs, kind):
+        copy = send(refs[0], refs[0], to_near, kind or "share", ("share", len(shared)))
+        shared.append((copy, refs[1], kind))
+
+    def offer(refs, kind=None):
+        hand_on(refs, kind)
+        share(refs, kind)
+
+    def forward(_):
+        for copy, twin, kind in shared:
             copy.wait_recv()
-            passed.append(send(twin, twin, frame_peer))
+            send(
+                twin,
+                twin,
+                frame_peer,
+                "pass late" if kind else "pass",
+                "late" if kind else "pass",
+            )
 
     ready = [finish(0, *piece) for piece in pieces]
     pass_on(2, 0, LATE)
     for refs in ready:
-        cross_over(refs)
-        share(refs)
+        offer(refs)
     for copy in sides:
         copy.wait_recv()
     start = jnp.concatenate([noise_buf[i] for i in range(F)], axis=1)
@@ -510,14 +544,12 @@
 
     ready = [finish(1, *piece) for piece in pieces]
     for refs in ready:
-        cross_over(refs)
-        share(refs)
+        offer(refs)
     ready = finish(2, 0, LATE)
     build(4, set_own, f)
 
     def share_rest(_):
-        cross_over(ready)
-        share(ready)
+        offer(ready, "late")
 
     hot_row = lax.broadcasted_iota(jnp.int32, (32 - C, N), 0)
     ones_rows = jnp.ones((C, N), BF16)
@@ -567,6 +599,7 @@
     spread = [key for act, key in PLAN if act == "spread"]
     local = [key for act, key in PLAN if act == "local"]
     state, local_eps, drift, flying = {}, {}, {}, {}
+    rounds_at = rsem.shape[0] - len(spread) - len(local)
     outward = sorted(
         range(1, 2 * PL), key=lambda d: (-(d // PL + (d % PL // H > 0)), -(d // PL))
     )
@@ -578,8 +611,7 @@
             x = x + drift[(min(i - 1, m), m)]
         state[key] = x
         part, local_eps[key] = evaluate(x, j, slots)
-        k = count[0]
-        count[0] += 1
+        k = flying[key] = len(flying)
         if key in spread:
             slot = plane_buf.at[spread.index(key), e * PL + q_me]
             slot[...] = part.astype(BF16)
@@ -592,23 +624,19 @@
             pltpu.make_async_remote_copy(
                 src_ref=slot,
                 dst_ref=slot,
-                send_sem=ssem.at[k],
-                recv_sem=rsem.at[k],
+                send_sem=ssem.at[spare[k]],
+                recv_sem=rsem.at[rounds_at + k],
                 device_id=peer,
                 device_id_type=MESH,
             ).start()
-        flying[key] = k
-
-    def settle(key, sem):
+
+    def land(key):
+        j, k = key[1], flying[key]
         if key in spread:
             others = plane_buf.at[spread.index(key), pl.ds(0, 2 * PL - 1)]
         else:
             others = chip_buf.at[local.index(key), 0]
-        pltpu.make_async_copy(others, others, sem).wait()
-
-    def land(key):
-        j, k = key[1], flying[key]
-        settle(key, rsem.at[k])
+        settle(others, rsem.at[rounds_at + k])
         total = local_eps[key]
         if key in spread:
             for i in range(2 * PL):
@@ -617,19 +645,32 @@
             for i in range(H):
                 total = total + chip_buf[local.index(key), i]
         drift[key] = keeps[j] * state[key] + coefs[j] * total
-        settle(key, ssem.at[k])
+        settle(others, ssem.at[spare[k]])
 
     def clear(_):
-        for copy in started:
-            copy.wait_send()
-        started.clear()
+        for out, ref in (
+            ("near", near_send.at[pl.ds(0, 2)]),
+            ("far", far_send.at[pl.ds(0, 2)]),
+            ("across", fin_qk.at[0]),
+            ("share", fin_qk.at[0]),
+            ("pass", fin_qk.at[0]),
+            ("late", fin_late),
+            ("pass late", fin_late.at[0]),
+            ("turn", at_peer),
+            ("meta", meta_buf.at[pl.ds(0, S - 1)]),
+            ("mix", mix_buf.at[pl.ds(0, S - 1)]),
+            ("noise", noise_buf.at[0]),
+            ("ends", ends_buf.at[0]),
+        ):
+            settle(ref, ssem.at[outs[out]])
 
     def gather(_):
         build(set_own, set_own, f)
         build(set_near, set_near, f)
-        for copies, member in ((across, e), (passed, e_near)):
-            for copy in copies:
-                copy.wait_recv()
+        arrive(fin_qk.at[0], "across")
+        arrive(fin_qk.at[0], "pass")
+        arrive(fin_late.at[pl.ds(0, 2)], "late")
+        for member in (e, e_near):
             twin = 2 * (1 - f) + member
             build(twin, twin, 1 - f)
 
@@ -678,13 +719,12 @@
 PLAN = (
     ("share", None),
     ("spread", (0, 0)),
-    ("forward", 6),
     ("spread", (0, 1)),
+    ("forward", None),
     ("land", (0, 0)),
-    ("forward", 1),
     ("spread", (1, 1)),
+    ("spread", (0, 2)),
     ("land", (0, 1)),
-    ("spread", (0, 2)),
     ("spread", (1, 2)),
     ("gather", None),
     ("clear", None),
@@ -726,7 +766,7 @@
     late = 2 * V + (QK + V) // 4
     n_spread = sum(act == "spread" for act, _ in PLAN)
     n_local = sum(act == "local" for act, _ in PLAN)
-    n_sems = 2 * (S - 1) + 3 + 5 * 7 + n_spread + n_local
+    n_evals = n_spread + n_local
     vmem = pl.BlockSpec(memory_space=pltpu.VMEM)
     smem = pl.BlockSpec(memory_space=pltpu.SMEM)
     here = pl.BlockSpec(memory_space=pl.ANY)
@@ -767,8 +807,8 @@
             pltpu.VMEM((S, 2 * C, N), F32),
             pltpu.VMEM((n_spread, 2 * PL, C, N), BF16),
             pltpu.VMEM((n_local, H, C, N), F32),
-            pltpu.SemaphoreType.DMA((n_sems + 12,)),
-            pltpu.SemaphoreType.DMA((n_sems,)),
+            pltpu.SemaphoreType.DMA((14 + 6 + n_evals - 8,)),
+            pltpu.SemaphoreType.DMA((3 * 7 + 8 + n_evals,)),
         ],
         compiler_params=pltpu.CompilerParams(
             collective_id=0, has_side_effects=True, vmem_limit_bytes=60 * 1024 * 1024

time: 35.6 us -> 35.2 us (0.989)
  Pallas kernels: 32.4 us -> 32 us
    pallas_call x1, Pallas kernels: 32.4 us -> 32 us  [local_heads(): pl.pallas_call(functools.partial(kernel, S, F, H), out_shape=(pltpu.VMEM(...]
where the time goes in v5:
time: 35.2 us; the launch traced here: 35 us
  Pallas kernels  32 us (91%)
  between operations  1.93 us (5%)
  local copies, waits for them, and re-layouts  1.11 us (3%)
    pallas_call x1, Pallas kernels, local_heads(): pl.pallas_call(functools.partial(kernel, S, F, H), out_shape=(pltpu.VMEM(...  32 us
    unnamed x2, local copies, waits for them, and re-layouts  1.11 us

profile of v5, /device:TPU:0, one launch (start us, length us, event | category | flops | bytes accessed | tf_op | source)
XLA Modules:
  0.0 35.0 jit_solution(6066499581176498787)
XLA Ops:
  1.9 32.0 %shard_map.131 = (f32[1,16,128]{2,1,0:T(8,128)S(1)}, f32[1,4]{1,0:T(1,128)S(1)}) custom-call(f32[16,128]{1,0:T(8,128)} %noise_hbm.1, bf16[128,1152]{1,0:T(8,128)(2,1)} %pos_hbm.1, bf16[128,1152]{1,0:T(8,128)(2,1)} %table_hbm.1, s32[1]{0:T(128)S(6)} %copy.18.tidx_ref, s32[1]{0:T(128)S(6)} %copy.19.sidx_ref, f32[1,128]{1,0:T(1,128)} %bitcast.6, ...), custom_call_target="tpu_custom_call" | custom-call | tf_op jit(solution)/shard_map/pallas_call | solution.py:773
  33.9 0.6 %copy.16 = f32[1,16,128]{2,1,0:T(8,128)} copy(f32[1,16,128]{2,1,0:T(8,128)S(1)} %get-tuple-element.6) | data formatting | bytes 16384
  34.5 0.5 %copy.17 = f32[4]{0:T(128)} copy(f32[4]{0:T(128)S(1)} %bitcast.4) | data formatting | bytes 32

commit v6 on v5

--- a/solution.py
+++ b/solution.py
@@ -395,7 +395,6 @@
 
     side_ref[0:C] = w_in.astype(F32)
     arrive(meta_buf.at[pl.ds(0, S - 1)], "meta")
-    arrive(mix_buf.at[pl.ds(0, S - 1)], "mix")
     metas = [meta_buf[j] for j in range(S)]
     hot = jnp.concatenate(
         [m[0:1] for m in metas] + [jnp.zeros((8 - S, lanes), F32)], axis=0
@@ -413,6 +412,12 @@
             side_cut[...] = (side_ref[:, cut] * gain[:, cut]).astype(BF16)
 
     side_mine = side_cut[...]
+    turned_of = []
+    for role, member in ((0, e), (1, e_near)):
+        turned = dot(wt_ref[member], side_mine, 1, 1)
+        pv_ref[role, :, 2 * rows : 2 * rows + 32] = turned[QK:].astype(BF16)
+        turned_of.append(turned[0:QK])
+    arrive(mix_buf.at[pl.ds(0, S - 1)], "mix")
     mix = mix_buf[0].astype(F32)
     for j in range(1, S):
         mix = mix + mix_buf[j].astype(F32)
@@ -420,8 +425,6 @@
     mix_row = lax.broadcasted_iota(jnp.int32, (V, B), 0) // C
 
     def late_rows(role, member):
-        turned = dot(wt_ref[member], side_mine, 1, 1)
-        pv_ref[role, :, 2 * rows : 2 * rows + 32] = turned[QK:].astype(BF16)
         part = jnp.where(member == 0, mix[:, 0:B], mix[:, B : 2 * B])
         block = jnp.where(
             mix_lane == mix_row, jnp.concatenate([part] * HZ, axis=0), 0.0
@@ -430,7 +433,7 @@
         values = dot(jnp.concatenate([block_hi, block_lo], axis=0), pv_ref[role])
         values = values[0:V] + values[V : 2 * V]
         packs = []
-        for arr in (turned[0:QK], values[:, 2 * rows : 2 * rows + 32]):
+        for arr in (turned_of[role], values[:, 2 * rows : 2 * rows + 32]):
             size = arr.shape[0] // 4
             packs.append(
                 jnp.concatenate([arr[g * size : (g + 1) * size] for g in range(4)], axis=1)
@@ -837,7 +840,10 @@
         and time_index.shape[0] == S
         and w_qkv.shape[2] == S * F * H * HDIM
         and w_qkv.shape[0] % (16 * S) == 0
-        and start_noise.shape[1] % (128 * F) == 0
+        and F == 2
+        and H == 2
+        and start_noise.shape[1] == 128 * F
+        and start_noise.shape[0] == 16 * mesh.shape["parts"]
         and start_noise.shape[1] // F <= time_table.shape[0]
         and time_table.shape[0] % 128 == 0
     )

time: 35.2 us -> 35.1 us (level)
  no operation moved by 1% of the time
where the time goes in v6:
time: 35.1 us; the launch traced here: 34.9 us
  Pallas kernels  31.9 us (91%)
  between operations  1.93 us (5%)
  local copies, waits for them, and re-layouts  1.11 us (3%)
    pallas_call x1, Pallas kernels, local_heads(): pl.pallas_call(functools.partial(kernel, S, F, H), out_shape=(pltpu.VMEM(...  31.9 us
    unnamed x2, local copies, waits for them, and re-layouts  1.11 us

profile of v6, /device:TPU:0, one launch (start us, length us, event | category | flops | bytes accessed | tf_op | source)
XLA Modules:
  0.0 34.9 jit_solution(584278366162402488)
XLA Ops:
  1.9 31.9 %shard_map.131 = (f32[1,16,128]{2,1,0:T(8,128)S(1)}, f32[1,4]{1,0:T(1,128)S(1)}) custom-call(f32[16,128]{1,0:T(8,128)} %noise_hbm.1, bf16[128,1152]{1,0:T(8,128)(2,1)} %pos_hbm.1, bf16[128,1152]{1,0:T(8,128)(2,1)} %table_hbm.1, s32[1]{0:T(128)S(6)} %copy.18.tidx_ref, s32[1]{0:T(128)S(6)} %copy.19.sidx_ref, f32[1,128]{1,0:T(1,128)} %bitcast.6, ...), custom_call_target="tpu_custom_call" | custom-call | tf_op jit(solution)/shard_map/pallas_call | solution.py:776
  33.8 0.6 %copy.16 = f32[1,16,128]{2,1,0:T(8,128)} copy(f32[1,16,128]{2,1,0:T(8,128)S(1)} %get-tuple-element.6) | data formatting | bytes 16384
  34.4 0.5 %copy.17 = f32[4]{0:T(128)} copy(f32[4]{0:T(128)S(1)} %bitcast.4) | data formatting | bytes 32

commit v7 on v6

--- a/solution.py
+++ b/solution.py
@@ -565,7 +565,7 @@
         out = jnp.zeros((C, N), F32)
         items, scores, r, eps = {}, {}, None, None
         G = len(slots)
-        for g in range(G + 2):
+        for g in range(G + 3):
             if g < G:
                 big = big_buf[slots[g]]
                 if g == 0:
@@ -586,16 +586,16 @@
                     k = lin[B + n * HDIM : B + (n + 1) * HDIM].astype(BF16)
                     v_hi, v_lo = two(lin[QK + n * C : QK + (n + 1) * C])
                     items[g, n] = q, k, jnp.concatenate([v_hi, v_lo, ones_rows], axis=0)
-            if 0 <= g - 1 < G:
-                for n in range(HZ):
-                    q, k, _ = items[g - 1, n]
-                    scores[g - 1, n] = dot(k, q, 0, 0)
             if 0 <= g - 2 < G:
                 for n in range(HZ):
-                    block = scores.pop((g - 2, n))
+                    q, k, _ = items[g - 2, n]
+                    scores[g - 2, n] = dot(k, q, 0, 0)
+            if 0 <= g - 3 < G:
+                for n in range(HZ):
+                    block = scores.pop((g - 3, n))
                     top = jnp.max(block, axis=0, keepdims=True)
                     p = jnp.exp2(block - top).astype(BF16)
-                    o = dot(items[g - 2, n][2], p)
+                    o = dot(items[g - 3, n][2], p)
                     out = out + (o[0:C] + o[C : 2 * C]) / o[2 * C : 2 * C + 1]
         return out, eps
 

time: 35.1 us -> 34.8 us (level)
  no operation moved by 1% of the time
where the time goes in v7:
time: 34.8 us; the launch traced here: 34.7 us
  Pallas kernels  31.6 us (91%)
  between operations  1.93 us (6%)
  local copies, waits for them, and re-layouts  1.11 us (3%)
    pallas_call x1, Pallas kernels, local_heads(): pl.pallas_call(functools.partial(kernel, S, F, H), out_shape=(pltpu.VMEM(...  31.6 us
    unnamed x2, local copies, waits for them, and re-layouts  1.11 us

profile of v7, /device:TPU:0, one launch (start us, length us, event | category | flops | bytes accessed | tf_op | source)
XLA Modules:
  0.0 34.7 jit_solution(14238710904487653753)
XLA Ops:
  1.9 31.6 %shard_map.131 = (f32[1,16,128]{2,1,0:T(8,128)S(1)}, f32[1,4]{1,0:T(1,128)S(1)}) custom-call(f32[16,128]{1,0:T(8,128)} %noise_hbm.1, bf16[128,1152]{1,0:T(8,128)(2,1)} %pos_hbm.1, bf16[128,1152]{1,0:T(8,128)(2,1)} %table_hbm.1, s32[1]{0:T(128)S(6)} %copy.18.tidx_ref, s32[1]{0:T(128)S(6)} %copy.19.sidx_ref, f32[1,128]{1,0:T(1,128)} %bitcast.6, ...), custom_call_target="tpu_custom_call" | custom-call | tf_op jit(solution)/shard_map/pallas_call | solution.py:776
  33.5 0.6 %copy.16 = f32[1,16,128]{2,1,0:T(8,128)} copy(f32[1,16,128]{2,1,0:T(8,128)S(1)} %get-tuple-element.6) | data formatting | bytes 16384
  34.1 0.5 %copy.17 = f32[4]{0:T(128)} copy(f32[4]{0:T(128)S(1)} %bitcast.4) | data formatting | bytes 32
